TPU v7x, 32 devices: a whole 2x2x4 slice. The times are simulated.
32 devices in a mesh: dp: 8 (over z, x), mp: 4 (over y, core).
Axes of the slice: x: 2, y: 2, z: 4, core: 2. Of those that a mesh axis runs over, the one named last changes fastest.
Arguments:
- vision_rows: bfloat16 [1024, 1024], P('dp'), may hold values from -6 to 6
- image_count: int32 [32], P('dp'), may hold values from 0 to 4
- proj_flat: bfloat16 [32768, 128], P(('dp', 'mp')), may hold values from -0.1875 to 0.1875
- text_embeds: bfloat16 [3072, 4096], P(('dp', 'mp')), may hold values from -6 to 6
- norm_gain: float32 [4096], replicated, may hold values from 0.1 to 1.9
- q_weight: bfloat16 [4096, 4096], P(None, 'mp'), may hold values from -0.09375 to 0.09375
- q_grad: bfloat16 [4096, 4096], P('dp', 'mp'), may hold values from -6 to 6
Outputs:
- text_grad: bfloat16 [3072, 4096], P(('dp', 'mp'))
- proj_grad: float32 [32768, 128], P(('dp', 'mp'))
Inputs may be any that keep to these rules, and one draw needn't show every extreme that they name: Slot s of device k holds an image when s < image_count[k]; other slots are padding.
All inputs are finite; a program needn't handle non-finite values.
Results may differ from a plain program's by a relative error of at most 0.014.
Values may be sent and summed in bfloat16 or wider, within the bound.
A program may use at most 64 MiB of HBM per device.

v0:
```python
import functools

import jax
import jax.numpy as jnp
from jax import lax
from jax.experimental import pallas as pl
from jax.experimental.pallas import tpu as pltpu
from jax.sharding import PartitionSpec as P

IMG_MAX = 4
PATCH = 8
ROWS_DEV = 128
CORES = 2
SIDE = 2
CHUNKS = 4
TURNED = 1
PIECES = 2
TILE = 256
ROW_STEP = 16

MESH = pl.DeviceIdType.MESH

norm_eps = 1e-05


def row_term(left, weight):
    return lax.dot_general(
        left, weight, (((1,), (1,)), ((), ())), preferred_element_type=jnp.float32
    )


class LineGather:
    def __init__(self, depth, me, member, own, buf, send, recv, turn):
        self.turn_send = turn
        self.depth, self.me, self.member = depth, me, member
        self.z, self.x = me // SIDE, me % SIDE
        self.own, self.buf, self.send, self.recv = own, buf, send, recv
        self.step = buf.shape[1] // CHUNKS

    def rows(self, chunk):
        return pl.ds(chunk * self.step, self.step)

    def copy(self, zz, x, chunk, way, own=False):
        block = zz * SIDE + x
        place = self.buf.at[block, self.rows(chunk)]
        target = (self.me + SIDE, self.me - SIDE, self.z * SIDE + (1 - self.x))[way]
        return pltpu.make_async_remote_copy(
            src_ref=self.own.at[self.rows(chunk)] if own else place,
            dst_ref=place,
            send_sem=self.send.at[way, zz, chunk],
            recv_sem=self.recv.at[block, chunk],
            device_id=(target, self.member),
            device_id_type=MESH,
        )

    def start(self):
        for chunk in range(CHUNKS):
            @pl.when(self.z < self.depth - 1)
            def _():
                self.copy(self.z, self.x, chunk, 0, True).start()

            @pl.when(self.z > 0)
            def _():
                self.copy(self.z, self.x, chunk, 1, True).start()

            self.copy(self.z, self.x, chunk, 2, True).start()

    def turned(self, way, chunk):
        block = (self.depth - 1 if way else 0) * SIDE + 1 - self.x
        place = self.buf.at[block, self.rows(chunk)]
        return pltpu.make_async_remote_copy(
            src_ref=place,
            dst_ref=place,
            send_sem=self.turn_send.at[way, chunk],
            recv_sem=self.recv.at[block, chunk],
            device_id=(self.me - SIDE if way else self.me + SIDE, self.member),
            device_id_type=MESH,
        )

    def turn(self, hop):
        last = self.depth - 1
        for way, place in ((0, self.z), (1, last - self.z)):
            due = (place == hop) | (place == 0) if hop == 1 else place == hop

            @pl.when(due)
            def _():
                for chunk in range(CHUNKS - TURNED, CHUNKS):
                    self.turned(way, chunk).wait_recv()

                    @pl.when(place < last)
                    def _():
                        self.turned(way, chunk).start()

    def relay(self, hop, chunk):
        below, above = self.z - hop, self.z + hop
        final = chunk >= CHUNKS - TURNED

        @pl.when(below >= 0)
        def _():
            self.copy(below, self.x, chunk, 0).wait_recv()

            @pl.when(self.z < self.depth - 1)
            def _():
                self.copy(below, self.x, chunk, 0).start()

            @pl.when(below > 0 if final else below >= 0)
            def _():
                self.copy(below, self.x, chunk, 2).start()

        @pl.when(above < self.depth)
        def _():
            self.copy(above, self.x, chunk, 1).wait_recv()

            @pl.when(self.z > 0)
            def _():
                self.copy(above, self.x, chunk, 1).start()

            @pl.when(above < self.depth - 1 if final else above < self.depth)
            def _():
                self.copy(above, self.x, chunk, 2).start()

        if chunk == CHUNKS - 1:
            self.turn(hop)

    def line_blocks(self, hop, use):
        for zz in (self.z - hop, self.z + hop):
            @pl.when((zz >= 0) & (zz < self.depth))
            def _():
                use(zz * SIDE + self.x)

    def side_blocks(self, hop, use):
        for zz in (self.z,) if hop == 0 else (self.z - hop, self.z + hop):
            @pl.when((zz >= 0) & (zz < self.depth))
            def _():
                for chunk in range(CHUNKS - TURNED):
                    self.copy(zz, 1 - self.x, chunk, 2).wait_recv()

                @pl.when((zz > 0) & (zz < self.depth - 1))
                def _():
                    for chunk in range(CHUNKS - TURNED, CHUNKS):
                        self.copy(zz, 1 - self.x, chunk, 2).wait_recv()

                use(zz * SIDE + 1 - self.x)

    def drain(self):
        for zz in range(self.depth):
            for chunk in range(CHUNKS):
                @pl.when((self.z >= zz) & (self.z < self.depth - 1))
                def _():
                    self.copy(zz, self.x, chunk, 0).wait_send()

                @pl.when((self.z <= zz) & (self.z > 0))
                def _():
                    self.copy(zz, self.x, chunk, 1).wait_send()

                if chunk >= CHUNKS - TURNED and zz in (0, self.depth - 1):
                    @pl.when(self.z == zz)
                    def _():
                        self.copy(zz, self.x, chunk, 2).wait_send()
                else:
                    self.copy(zz, self.x, chunk, 2).wait_send()
        for way, place in ((0, self.z), (1, self.depth - 1 - self.z)):
            @pl.when(place < self.depth - 1)
            def _():
                for chunk in range(CHUNKS - TURNED, CHUNKS):
                    self.turned(way, chunk).wait_send()


def kernel(
    shards, groups, grad_scale,
    proj_ref, vision_ref, count_ref, gain_ref, q_hbm, w_hbm, text_hbm,
    text_out, proj_out,
    qv, wv, tv, own_text, own_image, mate_text, mate_image, sum_text, sum_image,
    far_text, far_image, scaled_image, x_acc, g_acc, g_own, stat_own, stats,
    w_all, w_flat, g_all, v_all,
    q_sem, w_sem, t_sem, a_send, a_recv, a_turn, c_send, c_recv, c_turn, v_send, v_recv, vm_send, vm_recv,
    mt_send, mt_recv, mi_send, mi_recv, ft_send, ft_recv, fi_send, fi_recv, s_send, s_recv,
):
    me, member = lax.axis_index("dp"), lax.axis_index("mp")
    depth = shards // SIDE
    chips = groups // CORES
    y, core = member // CORES, member % CORES
    mate = y * CORES + 1 - core
    shard_k, block_cols = g_acc.shape
    fold = block_cols // 128
    image_rows = vision_ref.shape[0]
    per_image = image_rows // groups
    rows_dev = qv.shape[0] // groups
    text_rows = rows_dev - per_image
    width = groups * block_cols
    f32, bf16 = jnp.float32, jnp.bfloat16

    far = [lax.rem(y + step, chips) for step in range(1, chips)]
    order = [yy * CORES + lax.rem(core + flip, CORES) for yy in far + [y] for flip in (1, 0)]
    early = len(order) // 2

    q_copy = pltpu.make_async_copy(q_hbm, qv, q_sem)
    q_copy.start()
    w_copies = [pltpu.make_async_copy(w_hbm.at[j], wv.at[j], w_sem.at[k]) for k, j in enumerate(order)]
    for copy in w_copies:
        copy.start()
    t_copy = pltpu.make_async_copy(text_hbm, tv, t_sem)
    t_copy.start()

    barrier = pltpu.get_barrier_semaphore()
    z, x = me // SIDE, me % SIDE

    @pl.when(z > 0)
    def _():
        pl.semaphore_signal(barrier, inc=1, device_id=(me - SIDE, member), device_id_type=MESH)

    @pl.when(z < depth - 1)
    def _():
        pl.semaphore_signal(barrier, inc=1, device_id=(me + SIDE, member), device_id_type=MESH)

    across = z * SIDE + 1 - x
    pl.semaphore_signal(barrier, inc=1, device_id=(across, member), device_id_type=MESH)
    for step in range(1, groups):
        pl.semaphore_signal(
            barrier, inc=1, device_id=(me, lax.rem(member + step, groups)), device_id_type=MESH
        )
    @pl.when((z > 0) & (z < depth - 1))
    def _():
        pl.semaphore_wait(barrier, 2 + groups)

    @pl.when((z == 0) | (z == depth - 1))
    def _():
        pl.semaphore_wait(barrier, 1 + groups)

    weights = LineGather(depth, me, member, proj_ref, w_all, a_send, a_recv, a_turn)
    weights.start()

    def remote(src, dst, send, recv, device):
        return pltpu.make_async_remote_copy(
            src_ref=src, dst_ref=dst, send_sem=send, recv_sem=recv,
            device_id=device, device_id_type=MESH,
        )

    def text_to_mate(k):
        j = order[k]
        return remote(own_text.at[j, 1 - core], mate_text.at[j], mt_send.at[j], mt_recv.at[j], (me, mate))

    def image_to_mate(yy):
        return remote(
            own_image.at[yy * CORES + 1 - core], mate_image.at[yy],
            mi_send.at[yy], mi_recv.at[yy], (me, mate),
        )

    def text_to_far(k, yy):
        j = order[k]
        return remote(
            sum_text.at[j, yy], far_text.at[y, j], ft_send.at[j, yy], ft_recv.at[y, j],
            (me, yy * CORES + core),
        )

    def text_from_far(k, yy):
        j = order[k]
        return remote(
            sum_text.at[j, yy], far_text.at[yy, j], ft_send.at[j, yy], ft_recv.at[yy, j],
            (me, yy * CORES + core),
        )

    def image_to_far(yy):
        return remote(
            sum_image.at[yy], far_image.at[y], fi_send.at[yy], fi_recv.at[y], (me, yy * CORES + core)
        )

    def image_from_far(yy):
        return remote(
            sum_image.at[yy], far_image.at[yy], fi_send.at[yy], fi_recv.at[yy], (me, yy * CORES + core)
        )

    def multiply(k):
        j = order[k]
        w_copies[k].wait()

        @pl.loop(0, block_cols // TILE)
        def _(n):
            cols = pl.ds(pl.multiple_of(n * TILE, TILE), TILE)
            term = row_term(qv[...], wv[j, cols, :]).astype(bf16)
            for g in range(groups):
                base = g * rows_dev
                own_image[j, pl.ds(g * per_image, per_image), cols] = term[base : base + per_image]
                own_text[j, g % CORES, g // CORES, :, cols] = term[base + per_image : base + rows_dev]

        text_to_mate(k).start()

    def add_image(yy):
        image_to_mate(yy).wait_recv()

        @pl.loop(0, image_rows // ROW_STEP)
        def _(n):
            rows = pl.ds(pl.multiple_of(n * ROW_STEP, ROW_STEP), ROW_STEP)
            total = own_image[yy * CORES + core, rows].astype(f32) + mate_image[yy, rows].astype(f32)
            sum_image[yy, rows] = total.astype(bf16)

    def add_text(k):
        j = order[k]
        text_to_mate(k).wait_recv()
        for yy in far:
            @pl.loop(0, text_rows // ROW_STEP)
            def _(n):
                rows = pl.ds(pl.multiple_of(n * ROW_STEP, ROW_STEP), ROW_STEP)
                total = own_text[j, core, yy, rows].astype(f32) + mate_text[j, yy, rows].astype(f32)
                sum_text[j, yy, rows] = total.astype(bf16)

    def send_text(k):
        for yy in far:
            text_to_far(k, yy).start()

    q_copy.wait()
    for k in range(early):
        multiply(k)
        if k % CORES == 0:
            image_to_mate(far[k // CORES]).start() if k // CORES < len(far) else None
    for yy in far[: early // CORES]:
        add_image(yy)
        image_to_far(yy).start()
    weights.relay(1, 0)
    for k in range(early):
        add_text(k)
        send_text(k)
    for chunk in range(1, CHUNKS):
        weights.relay(1, chunk)
    for k in range(early, len(order)):
        multiply(k)
        if k % CORES == 0:
            image_to_mate((far + [y])[k // CORES]).start()
        if 2 < depth and k - early < CHUNKS:
            weights.relay(2, k - early)
    for yy in far[early // CORES :]:
        add_image(yy)
        image_to_far(yy).start()
    for chunk in range(len(order) - early, CHUNKS):
        weights.relay(2, chunk)

    def wide(shard):
        w_flat[...] = shard[...].astype(f32)
        parts = [w_flat[pl.ds(c, shard_k, stride=fold), :] for c in range(fold)]
        return jnp.concatenate(parts, axis=1).astype(bf16)

    def use_weights(block):
        cols = pl.ds(pl.multiple_of(block * shard_k, shard_k), shard_k)
        x_acc[...] += jnp.dot(vision_ref[:, cols], wide(w_all.at[block]), preferred_element_type=f32)

    own_cols = pl.ds(pl.multiple_of(me * shard_k, shard_k), shard_k)
    x_acc[...] = jnp.dot(vision_ref[:, own_cols], wide(proj_ref), preferred_element_type=f32)
    weights.line_blocks(1, use_weights)
    for hop in range(3, depth):
        for chunk in range(CHUNKS):
            weights.relay(hop, chunk)
    for hop in range(2, depth):
        weights.line_blocks(hop, use_weights)

    half = image_rows // CORES
    my_half = pl.ds(pl.multiple_of(core * half, half), half)
    mate_half = pl.ds(pl.multiple_of((1 - core) * half, half), half)

    def vision_to(step):
        target = lax.rem(me + step, shards)
        cols = pl.ds(pl.multiple_of(target * shard_k, shard_k), shard_k)
        return remote(
            vision_ref.at[my_half, cols], v_all.at[me, my_half],
            v_send.at[target], v_recv.at[me], (target, member),
        )

    def vision_from(step):
        source = lax.rem(me + step, shards)
        cols = pl.ds(pl.multiple_of(source * shard_k, shard_k), shard_k)
        return remote(
            vision_ref.at[my_half, cols], v_all.at[source, my_half],
            v_send.at[source], v_recv.at[source], (source, member),
        )

    def vision_to_mate(source):
        place = v_all.at[source, my_half]
        return remote(place, place, vm_send.at[source], vm_recv.at[source], (me, mate))

    def vision_from_mate(source):
        place = v_all.at[source, mate_half]
        return remote(place, place, vm_send.at[source], vm_recv.at[source], (me, mate))

    image_to_mate(y).wait_recv()
    for yy in far:
        image_from_far(yy).wait_recv()
    member_cols = pl.ds(pl.multiple_of(member * block_cols, block_cols), block_cols)

    @pl.loop(0, image_rows // ROW_STEP)
    def _(n):
        rows = pl.ds(pl.multiple_of(n * ROW_STEP, ROW_STEP), ROW_STEP)
        total = own_image[member, rows].astype(f32) + mate_image[y, rows].astype(f32)
        for yy in far:
            total = total + far_image[yy, rows].astype(f32)
        scaled_image[rows] = gain_ref[:, member_cols] * total

    for k in range(early, len(order)):
        add_text(k)
    for hop in range(depth):
        weights.side_blocks(hop, use_weights)
    for step in range(1, shards):
        vision_to(step).start()

    @pl.loop(0, image_rows // ROW_STEP)
    def _(n):
        rows = pl.ds(pl.multiple_of(n * ROW_STEP, ROW_STEP), ROW_STEP)
        x = x_acc[rows].astype(bf16).astype(f32)
        x_acc[rows] = x
        squares = jnp.sum(x * x, axis=1, keepdims=True)
        inner = jnp.sum(x * scaled_image[rows], axis=1, keepdims=True)
        lane = lax.broadcasted_iota(jnp.int32, (ROW_STEP, 128), 1)
        g_acc[rows, pl.ds(0, 128)] = jnp.where(lane == 0, squares, inner)

    stat_own[...] = g_acc[:, 0:128].T[0:8]

    def stat_to(step):
        target = lax.rem(member + step, groups)
        return remote(stat_own, stats.at[member], s_send.at[target], s_recv.at[member], (me, target))

    def stat_from(step):
        source = lax.rem(member + step, groups)
        return remote(stat_own, stats.at[source], s_send.at[source], s_recv.at[source], (me, source))

    for step in range(1, groups):
        stat_to(step).start()
    for k in range(early, len(order)):
        send_text(k)
    total = stat_own[...]
    for step in range(1, groups):
        stat_from(step).wait_recv()
        total = total + stats[lax.rem(member + step, groups)]
    spread = jnp.concatenate([total] * 16, axis=0).T
    inv_all = lax.rsqrt(spread[:, 0:1] / width + norm_eps)
    g_acc[:, 0:128] = jnp.broadcast_to(inv_all, (image_rows, 128))
    g_acc[:, 128:256] = jnp.broadcast_to(inv_all**3 * (spread[:, 1:2] / width), (image_rows, 128))

    for g in range(groups):
        held = count_ref[g] * PATCH

        @pl.loop(0, per_image // ROW_STEP)
        def _(n):
            first = n * ROW_STEP
            rows = pl.ds(pl.multiple_of(g * per_image + first, ROW_STEP), ROW_STEP)
            inv, pull = g_acc[rows, pl.ds(0, 1)], g_acc[rows, pl.ds(128, 1)]
            grad = inv * scaled_image[rows] - x_acc[rows] * pull
            slots = first + lax.broadcasted_iota(jnp.int32, (ROW_STEP, block_cols), 0)
            g_own[rows] = jnp.where(slots < held, grad, 0.0).astype(bf16)

    grads = LineGather(depth, me, member, g_own, g_all, c_send, c_recv, c_turn)
    grads.start()

    def vision_term(left, right):
        return lax.dot_general(left, right, (((0,), (0,)), ((), ())), preferred_element_type=f32)

    def use_grads(block):
        vision_from_mate(block).wait_recv()
        g_acc[...] += vision_term(v_all[block], g_all[block])

    g_acc[...] = vision_term(vision_ref[:, own_cols], g_own[...])
    for step in range(1, shards):
        vision_from(step).wait_recv()
        vision_to_mate(lax.rem(me + step, shards)).start()
    for hop in range(1, depth):
        for chunk in range(CHUNKS):
            grads.relay(hop, chunk)
        if hop < depth - 1:
            grads.line_blocks(hop, use_grads)
    grads.line_blocks(depth - 1, use_grads)

    for k in range(len(order)):
        for yy in far:
            text_from_far(k, yy).wait_recv()
    t_copy.wait()

    @pl.loop(0, text_rows // ROW_STEP)
    def _(n):
        rows = pl.ds(pl.multiple_of(n * ROW_STEP, ROW_STEP), ROW_STEP)
        squares = jnp.zeros((ROW_STEP, 1), f32)
        inner = jnp.zeros((ROW_STEP, 1), f32)
        for j in range(groups):
            cols = pl.ds(j * block_cols, block_cols)
            x = tv[rows, cols].astype(f32)
            norm = own_text[j, core, y, rows].astype(f32) + mate_text[j, y, rows].astype(f32)
            for yy in far:
                norm = norm + far_text[yy, j, rows].astype(f32)
            scaled = gain_ref[:, cols] * norm
            squares += jnp.sum(x * x, axis=1, keepdims=True)
            inner += jnp.sum(x * scaled, axis=1, keepdims=True)
        inv = lax.rsqrt(squares / width + norm_eps)
        pull = inv**3 * (inner / width)
        for j in range(groups):
            cols = pl.ds(j * block_cols, block_cols)
            x = tv[rows, cols].astype(f32)
            norm = own_text[j, core, y, rows].astype(f32) + mate_text[j, y, rows].astype(f32)
            for yy in far:
                norm = norm + far_text[yy, j, rows].astype(f32)
            text_out[rows, cols] = (inv * (gain_ref[:, cols] * norm) - x * pull).astype(bf16)

    for hop in range(depth):
        grads.side_blocks(hop, use_grads)
    for c in range(fold):
        proj_out[pl.ds(c, shard_k, stride=fold), :] = g_acc[:, c * 128 : (c + 1) * 128] * grad_scale

    weights.drain()
    grads.drain()
    for step in range(1, shards):
        vision_to(step).wait_send()
        vision_to_mate(lax.rem(me + step, shards)).wait_send()
    for step in range(1, groups):
        stat_to(step).wait_send()
    for k in range(len(order)):
        text_to_mate(k).wait_send()
        for yy in far:
            text_to_far(k, yy).wait_send()
    for yy in far + [y]:
        image_to_mate(yy).wait_send()
    for yy in far:
        image_to_far(yy).wait_send()


def place_outputs(text_in, proj_in, text_out, proj_out, text_held, proj_held, in_sem, out_sem):
    def copies(refs, sem):
        found = []
        for k, (src, dst) in enumerate(refs):
            step = src.shape[0] // PIECES
            for p in range(PIECES):
                rows = pl.ds(p * step, step)
                found.append(pltpu.make_async_copy(src.at[rows], dst.at[rows], sem.at[k, p]))
        return found

    into = copies(((text_in, text_held), (proj_in, proj_held)), in_sem)
    back = copies(((text_held, text_out), (proj_held, proj_out)), out_sem)
    for copy in into:
        copy.start()
    for first, second in zip(into, back):
        first.wait()
        second.start()
    for copy in back:
        copy.wait()


def live_rows(image_count, groups):
    image_rows = IMG_MAX * PATCH
    row_ids = jnp.arange(groups * image_rows, dtype=jnp.int32)
    owners = row_ids // image_rows
    slot_ids = row_ids % image_rows // PATCH
    owner_match = owners[:, None] == jnp.arange(groups, dtype=jnp.int32)[None, :]
    owner_counts = jnp.sum(jnp.where(owner_match, image_count[None, :], 0), axis=1)
    return (slot_ids < owner_counts)[:, None]


def fused_body(vision_rows, image_count, proj_flat, text_embeds, norm_gain, q_weight, q_grad):
    groups, shards = lax.axis_size("mp"), lax.axis_size("dp")
    model_width, bc = q_weight.shape
    image_rows, enc_width = vision_rows.shape
    text_rows = text_embeds.shape[0]
    shard_k = proj_flat.shape[0] * proj_flat.shape[1] // bc
    chips, depth = groups // CORES, shards // SIDE
    grad_scale = 1.0 / float(shards * image_rows) ** 0.5
    f32, bf16 = jnp.float32, jnp.bfloat16
    vmem, dma = pltpu.VMEM, pltpu.SemaphoreType.DMA
    on_chip = pl.BlockSpec(memory_space=pltpu.VMEM)
    scalars = pl.BlockSpec(memory_space=pltpu.SMEM)
    anywhere = pl.BlockSpec(memory_space=pl.ANY)
    text_grad, proj_block = pl.pallas_call(
        functools.partial(kernel, shards, groups, grad_scale),
        name="projector_backward",
        out_shape=(
            jax.ShapeDtypeStruct(text_embeds.shape, bf16),
            jax.ShapeDtypeStruct(proj_flat.shape, f32),
        ),
        in_specs=[on_chip, on_chip, scalars, on_chip] + [anywhere] * 3,
        out_specs=(on_chip, on_chip),
        scratch_shapes=[
            vmem(q_grad.shape, bf16),
            vmem((groups, bc, bc), bf16),
            vmem(text_embeds.shape, bf16),
            vmem((groups, CORES, chips, text_rows, bc), bf16),
            vmem((groups, image_rows, bc), bf16),
            vmem((groups, chips, text_rows, bc), bf16),
            vmem((chips, image_rows, bc), bf16),
            vmem((groups, chips, text_rows, bc), bf16),
            vmem((chips, image_rows, bc), bf16),
            vmem((chips, groups, text_rows, bc), bf16),
            vmem((chips, image_rows, bc), bf16),
            vmem((image_rows, bc), f32),
            vmem((image_rows, bc), f32),
            vmem((shard_k, bc), f32),
            vmem((image_rows, bc), bf16),
            vmem((8, image_rows), f32),
            vmem((groups, 8, image_rows), f32),
            vmem((shards,) + proj_flat.shape, bf16),
            vmem(proj_flat.shape, f32),
            vmem((shards, image_rows, bc), bf16),
            vmem((shards, image_rows, shard_k), bf16),
            dma, dma((groups,)), dma,
            dma((3, depth, CHUNKS)), dma((shards, CHUNKS)), dma((2, CHUNKS)),
            dma((3, depth, CHUNKS)), dma((shards, CHUNKS)), dma((2, CHUNKS)),
            dma((shards,)), dma((shards,)), dma((shards,)), dma((shards,)),
            dma((groups,)), dma((groups,)),
            dma((chips,)), dma((chips,)),
            dma((groups, chips)), dma((chips, groups)),
            dma((chips,)), dma((chips,)),
            dma((groups,)), dma((groups,)),
        ],
        compiler_params=pltpu.CompilerParams(
            collective_id=0, has_side_effects=True, vmem_limit_bytes=56 * 1024 * 1024
        ),
    )(
        proj_flat,
        vision_rows,
        image_count,
        norm_gain[None, :],
        q_grad,
        q_weight.reshape(groups, bc, bc),
        text_embeds,
    )
    kinds = (text_grad, proj_block)
    return pl.pallas_call(
        place_outputs,
        name="place_outputs",
        out_shape=tuple(jax.ShapeDtypeStruct(a.shape, a.dtype) for a in kinds),
        in_specs=[anywhere] * 2,
        out_specs=(anywhere, anywhere),
        scratch_shapes=[vmem(a.shape, a.dtype) for a in kinds] + [dma((2, PIECES)), dma((2, PIECES))],
    )(*kinds)


def norm_back(rows_in, grads, gain):
    inputs = rows_in.astype(jnp.float32)
    inv_rms = lax.rsqrt(jnp.mean(inputs * inputs, axis=-1, keepdims=True) + norm_eps)
    scaled = gain[None, :] * grads
    inner_mean = jnp.mean(scaled * inputs, axis=-1, keepdims=True)
    return inv_rms * scaled - inputs * inv_rms**3 * inner_mean


def general_body(vision_rows, image_count, proj_flat, text_embeds, norm_gain, q_weight, q_grad):
    groups = lax.axis_size("mp")
    member = lax.axis_index("mp")
    shards = lax.axis_size("dp")
    enc_width = vision_rows.shape[1]
    block_cols = q_weight.shape[1]
    model_width = q_weight.shape[0]
    used_count = enc_width * block_cols
    image_rows = IMG_MAX * PATCH
    gathered = lax.all_gather(proj_flat, "dp", axis=0, tiled=True)
    proj_block = gathered.reshape(-1)[:used_count].reshape(enc_width, block_cols)
    embed_cols = jnp.dot(vision_rows, proj_block, preferred_element_type=jnp.float32).astype(
        jnp.bfloat16
    )
    live_group = live_rows(image_count, groups)
    blocks = q_grad.reshape(groups, ROWS_DEV, block_cols)
    image_query = blocks[:, :image_rows].reshape(-1, block_cols)
    text_query = blocks[:, image_rows:].reshape(-1, block_cols)
    image_term = row_term(image_query, q_weight)
    image_norm = lax.psum_scatter(
        image_term.astype(jnp.bfloat16), "mp", scatter_dimension=1, tiled=True
    ).astype(jnp.float32)
    text_norm = lax.psum_scatter(
        row_term(text_query, q_weight).astype(jnp.bfloat16), "mp", scatter_dimension=0, tiled=True
    ).astype(jnp.float32)
    x_cols = embed_cols.astype(jnp.float32)
    gain_cols = lax.dynamic_slice_in_dim(norm_gain, member * block_cols, block_cols)
    scaled = gain_cols[None, :] * image_norm
    squares, inner_sum = lax.psum(
        (jnp.sum(x_cols * x_cols, axis=1), jnp.sum(scaled * x_cols, axis=1)), "mp"
    )
    inv_rms = lax.rsqrt(squares / model_width + norm_eps)[:, None]
    image_input = inv_rms * scaled - x_cols * inv_rms**3 * (inner_sum / model_width)[:, None]
    image_cols = jnp.where(live_group, image_input, 0.0).astype(jnp.bfloat16)
    text_grad = norm_back(text_embeds, text_norm, norm_gain).astype(jnp.bfloat16)
    grad_scale = 1.0 / jnp.sqrt(jnp.float32(shards * groups * image_rows))
    proj_part = (
        lax.dot_general(
            vision_rows, image_cols, (((0,), (0,)), ((), ())), preferred_element_type=jnp.float32
        )
        * grad_scale
    )
    stored_rows = proj_flat.shape[0]
    padded = jnp.pad(proj_part.reshape(-1), (0, shards * stored_rows * 128 - used_count))
    padded = padded.reshape(shards * stored_rows, 128)
    proj_grad = lax.psum_scatter(padded, "dp", scatter_dimension=0, tiled=True)
    return (text_grad, proj_grad)


def body(vision_rows, image_count, proj_flat, text_embeds, norm_gain, q_weight, q_grad):
    groups, shards = lax.axis_size("mp"), lax.axis_size("dp")
    bc = q_weight.shape[1]
    count = proj_flat.shape[0] * proj_flat.shape[1]
    shard_k = count // bc
    fits = (
        count % bc == 0
        and shard_k % 128 == 0
        and shard_k * shards == vision_rows.shape[1]
        and shard_k == vision_rows.shape[0]
        and bc % TILE == 0
        and groups > CORES
        and groups % CORES == 0
        and vision_rows.shape[0] // groups % ROW_STEP == 0
        and text_embeds.shape[0] % (PIECES * ROW_STEP) == 0
        and shards > SIDE
        and shards % SIDE == 0
    )
    run = fused_body if fits else general_body
    return run(vision_rows, image_count, proj_flat, text_embeds, norm_gain, q_weight, q_grad)


def solution(mesh):
    return jax.shard_map(
        body,
        mesh=mesh,
        in_specs=(
            P("dp", None),
            P("dp"),
            P(("dp", "mp"), None),
            P(("dp", "mp"), None),
            P(),
            P(None, "mp"),
            P("dp", "mp"),
        ),
        out_specs=(P(("dp", "mp"), None), P(("dp", "mp"), None)),
        check_vma=False,
    )
```

profile of v0, /device:TPU:0, one launch (start us, length us, event | category | flops | bytes accessed | tf_op | source)
XLA Modules:
  0.0 62.7 jit_solution(3424985974982901757)
XLA Ops:
  0.6 60.0 %projector_backward.1 = (bf16[96,4096]{1,0:T(8,128)(2,1)}, f32[1024,128]{1,0:T(8,128)}) custom-call(bf16[1024,128]{1,0:T(8,128)(2,1)} %proj_ref.1, bf16[128,1024]{1,0:T(8,128)(2,1)} %vision_ref.1, s32[4]{0:T(128)} %count_ref.1, f32[1,4096]{1,0:T(1,128)} %bitcast.3, bf16[512,1024]{1,0:T(8,128)(2,1)} %q_hbm.1, bf16[4,1024,1024]{2,1,0:T(8,128)(2,1)} %bitcast.2, ...), custom_call_target="tpu_custom_call" | custom-call | tf_op jit(solution)/shard_map/projector_backward/pallas_call | solution.py:564
  60.6 2.1 %place_outputs.1 = (bf16[96,4096]{1,0:T(8,128)(2,1)}, f32[1024,128]{1,0:T(8,128)}) custom-call(bf16[96,4096]{1,0:T(8,128)(2,1)} %get-tuple-element.4.text_in, f32[1024,128]{1,0:T(8,128)} %get-tuple-element.5.proj_in), custom_call_target="tpu_custom_call" | custom-call | tf_op jit(solution)/shard_map/place_outputs/pallas_call | solution.py:618
where the time goes:
time: 62.9 us; the launch traced here: 62.7 us
  Pallas kernels  62.1 us (99%)
  between operations  0.64 us (1%)
    pallas_call x1, Pallas kernels, fused_body(): pl.pallas_call(functools.partial(kernel, shards, groups, grad_scale), nam...  60 us
    pallas_call x1, Pallas kernels, fused_body(): pl.pallas_call(place_outputs, name='place_outputs', out_shape=tuple((jax....  2.11 us

commit v1 on v0

v1 whole, which is shorter than its diff:
```python
import functools

import jax
import jax.numpy as jnp
from jax import lax
from jax.experimental import pallas as pl
from jax.experimental.pallas import tpu as pltpu
from jax.sharding import PartitionSpec as P

IMG_MAX = 4
PATCH = 8
ROWS_DEV = 128
CORES = 2
SIDE = 2
CHUNKS = 4
PIECES = 2
LANES = 128
TILE = 256
ROW_STEP = 16

MESH = pl.DeviceIdType.MESH

norm_eps = 1e-05


def row_term(left, weight):
    return lax.dot_general(
        left, weight, (((1,), (1,)), ((), ())), preferred_element_type=jnp.float32
    )


def remote(src, dst, send, recv, device):
    return pltpu.make_async_remote_copy(
        src_ref=src, dst_ref=dst, send_sem=send, recv_sem=recv,
        device_id=device, device_id_type=MESH,
    )


class VisionGather:
    def __init__(self, depth, me, member, buf, block_rows, send, recv, mate_send, mate_recv):
        self.depth, self.me, self.member = depth, me, member
        self.z, self.x = me // SIDE, me % SIDE
        self.core = member % CORES
        self.mate = member + 1 - 2 * self.core
        self.buf, self.block_rows = buf, block_rows
        self.send, self.recv = send, recv
        self.mate_send, self.mate_recv = mate_send, mate_recv
        self.half = block_rows // CORES
        self.step = self.half // CHUNKS

    def place(self, block, chunk, core):
        first = block * self.block_rows + core * self.half + chunk * self.step
        return self.buf.at[pl.ds(pl.multiple_of(first, self.step), self.step)]

    def copy(self, zz, x, chunk, way):
        block = zz * SIDE + x
        place = self.place(block, chunk, self.core)
        target = (self.me + SIDE, self.me - SIDE, self.z * SIDE + 1 - self.x)[way]
        return remote(
            place, place, self.send.at[way, zz, chunk], self.recv.at[block, chunk],
            (target, self.member),
        )

    def to_mate(self, block, chunk):
        place = self.place(block, chunk, self.core)
        return remote(
            place, place, self.mate_send.at[block, chunk], self.mate_recv.at[block, chunk],
            (self.me, self.mate),
        )

    def from_mate(self, block, chunk):
        place = self.place(block, chunk, 1 - self.core)
        return remote(
            place, place, self.mate_send.at[block, chunk], self.mate_recv.at[block, chunk],
            (self.me, self.mate),
        )

    def start(self):
        for chunk in range(CHUNKS):
            @pl.when(self.z < self.depth - 1)
            def _():
                self.copy(self.z, self.x, chunk, 0).start()

            @pl.when(self.z > 0)
            def _():
                self.copy(self.z, self.x, chunk, 1).start()

            self.copy(self.z, self.x, chunk, 2).start()

    def relay(self, hop, chunk):
        below, above = self.z - hop, self.z + hop

        @pl.when(below >= 0)
        def _():
            self.copy(below, self.x, chunk, 0).wait_recv()

            @pl.when(self.z < self.depth - 1)
            def _():
                self.copy(below, self.x, chunk, 0).start()

            self.copy(below, self.x, chunk, 2).start()
            self.to_mate(below * SIDE + self.x, chunk).start()

        @pl.when(above < self.depth)
        def _():
            self.copy(above, self.x, chunk, 1).wait_recv()

            @pl.when(self.z > 0)
            def _():
                self.copy(above, self.x, chunk, 1).start()

            self.copy(above, self.x, chunk, 2).start()
            self.to_mate(above * SIDE + self.x, chunk).start()

    def levels(self, hop, use):
        for zz in (self.z,) if hop == 0 else (self.z - hop, self.z + hop):
            @pl.when((zz >= 0) & (zz < self.depth))
            def _():
                use(zz)

    def side(self, hop, chunk):
        def take(zz):
            self.copy(zz, 1 - self.x, chunk, 2).wait_recv()
            self.to_mate(zz * SIDE + 1 - self.x, chunk).start()

        self.levels(hop, take)

    def arrive(self, zz):
        for chunk in range(CHUNKS):
            @pl.when(zz != self.z)
            def _():
                self.from_mate(zz * SIDE + self.x, chunk).wait_recv()

            self.from_mate(zz * SIDE + 1 - self.x, chunk).wait_recv()

    def drain(self):
        for zz in range(self.depth):
            for chunk in range(CHUNKS):
                @pl.when((self.z >= zz) & (self.z < self.depth - 1))
                def _():
                    self.copy(zz, self.x, chunk, 0).wait_send()

                @pl.when((self.z <= zz) & (self.z > 0))
                def _():
                    self.copy(zz, self.x, chunk, 1).wait_send()

                self.copy(zz, self.x, chunk, 2).wait_send()

                @pl.when(zz != self.z)
                def _():
                    self.to_mate(zz * SIDE + self.x, chunk).wait_send()

                self.to_mate(zz * SIDE + 1 - self.x, chunk).wait_send()


def kernel(
    shards, groups, grad_scale,
    count_ref, proj_hbm, vision_hbm, gain_hbm, q_hbm, w_hbm, text_hbm,
    text_hbm_out, proj_out,
    pv, vv, gain_ref, q_image, q_text, wv, tv, text_out,
    own_text, own_image, mate_text, mate_image, sum_text, sum_image,
    far_text, far_image, w_flat, w_out, wt, n_out, nt, xt, gt, gain_t, o_out, o_in,
    stat_own, stat_near, stat_sum, stat_far,
    p_sem, vis_sem, gain_sem, q_sem, w_sem, t_sem, to_sem,
    v_send, v_recv, vm_send, vm_recv, wt_send, wt_recv, n_send, n_recv, o_send, o_recv,
    mt_send, mt_recv, mi_send, mi_recv, ft_send, ft_recv, fi_send, fi_recv,
    s_send, s_recv, z_send, z_recv,
):
    me, member = lax.axis_index("dp"), lax.axis_index("mp")
    depth = shards // SIDE
    chips = groups // CORES
    y, core = member // CORES, member % CORES
    mate = y * CORES + 1 - core
    z, x = me // SIDE, me % SIDE
    bc = wv.shape[1]
    span = bc // shards
    fold = bc // LANES
    shard_k = wt.shape[1] // shards
    image_rows = q_image.shape[0]
    per_image = image_rows // groups
    text_rows = tv.shape[0]
    rows_dev = per_image + text_rows
    width = groups * bc
    f32, bf16 = jnp.float32, jnp.bfloat16

    far = [lax.rem(y + step, chips) for step in range(1, chips)]
    order = [yy * CORES + lax.rem(core + flip, CORES) for yy in far + [y] for flip in (1, 0)]
    early = len(order) - CORES
    offsets = sorted(range(1, depth), key=lambda o: -min(o, depth - o)) + [0]
    targets = [
        lax.rem(z + o, depth) * SIDE + (x if flip else 1 - x) for o in offsets for flip in (0, 1)
    ]
    levels = [lax.rem(z + o, depth) for o in offsets]
    last = shards - 1

    p_copy = pltpu.make_async_copy(proj_hbm, pv, p_sem)
    p_copy.start()
    own_rows = pl.ds(pl.multiple_of(me * image_rows, image_rows), image_rows)
    vis_copy = pltpu.make_async_copy(vision_hbm, vv.at[own_rows], vis_sem)
    vis_copy.start()
    q_copies = []
    for g in range(groups):
        q_copies.append(pltpu.make_async_copy(
            q_hbm.at[pl.ds(g * rows_dev, per_image)],
            q_image.at[pl.ds(g * per_image, per_image)], q_sem.at[0, g],
        ))
    for g in range(groups):
        q_copies.append(pltpu.make_async_copy(
            q_hbm.at[pl.ds(g * rows_dev + per_image, text_rows)],
            q_text.at[pl.ds(g * text_rows, text_rows)], q_sem.at[1, g],
        ))
    w_copies = [pltpu.make_async_copy(w_hbm.at[j], wv.at[j], w_sem.at[k]) for k, j in enumerate(order)]
    for copy in q_copies[:groups] + w_copies[:1] + q_copies[groups:] + w_copies[1:]:
        copy.start()
    gain_copy = pltpu.make_async_copy(gain_hbm, gain_ref, gain_sem)
    gain_copy.start()
    t_copy = pltpu.make_async_copy(text_hbm, tv, t_sem)
    t_copy.start()

    barrier = pltpu.get_barrier_semaphore()
    across = z * SIDE + 1 - x
    beside = [(me, lax.rem(member + step, groups)) for step in range(1, groups)]
    beside += [(across, lax.rem(member + step, groups)) for step in range(groups)]
    peers = [(lax.rem(me + SIDE * o, shards), member) for o in range(1, depth)]
    peers += [(lax.rem(across + SIDE * o, shards), member) for o in range(1, depth)]
    for device in beside + peers:
        pl.semaphore_signal(barrier, inc=1, device_id=device, device_id_type=MESH)

    p_copy.wait()
    w_flat[...] = pv[...].astype(f32)
    for j in range(shards):
        w_out[j] = w_flat[pl.ds(j, shard_k, stride=fold), :].T.astype(bf16)
    own_k = pl.ds(pl.multiple_of(me * shard_k, shard_k), shard_k)
    wt[:, own_k] = w_out[me]
    vis_copy.wait()

    pl.semaphore_wait(barrier, len(beside) + len(peers))

    vision = VisionGather(depth, me, member, vv, image_rows, v_send, v_recv, vm_send, vm_recv)
    vision.start()

    def w_to(t):
        j = targets[t]
        return remote(w_out.at[j], wt.at[:, own_k], wt_send.at[t], wt_recv.at[me], (j, member))

    def w_from(t):
        j = targets[t]
        cols = pl.ds(pl.multiple_of(j * shard_k, shard_k), shard_k)
        return remote(w_out.at[j], wt.at[:, cols], wt_send.at[t], wt_recv.at[j], (j, member))

    for t in range(last):
        w_to(t).start()

    def text_to_mate(k):
        j = order[k]
        return remote(own_text.at[j, 1 - core], mate_text.at[j], mt_send.at[j], mt_recv.at[j], (me, mate))

    def image_to_mate(yy):
        return remote(
            own_image.at[yy * CORES + 1 - core], mate_image.at[yy],
            mi_send.at[yy], mi_recv.at[yy], (me, mate),
        )

    def text_to_far(k, yy):
        j = order[k]
        return remote(
            sum_text.at[j, yy], far_text.at[y, j], ft_send.at[j, yy], ft_recv.at[y, j],
            (me, yy * CORES + core),
        )

    def text_from_far(k, yy):
        j = order[k]
        return remote(
            sum_text.at[j, yy], far_text.at[yy, j], ft_send.at[j, yy], ft_recv.at[yy, j],
            (me, yy * CORES + core),
        )

    def piece(t):
        return pl.ds(pl.multiple_of(targets[t] * span, span), span)

    def image_to_far(yy, t):
        return remote(
            sum_image.at[yy, piece(t)], far_image.at[y, piece(t)],
            fi_send.at[yy, t], fi_recv.at[y, t], (me, yy * CORES + core),
        )

    def image_from_far(yy, t):
        return remote(
            sum_image.at[yy, piece(t)], far_image.at[yy, piece(t)],
            fi_send.at[yy, t], fi_recv.at[yy, t], (me, yy * CORES + core),
        )

    def image_multiply(k):
        j = order[k]
        w_copies[k].wait()

        @pl.loop(0, bc // TILE)
        def _(n):
            rows = pl.ds(pl.multiple_of(n * TILE, TILE), TILE)
            own_image[j, rows] = row_term(wv[j, rows], q_image[...]).astype(bf16)

        if k % CORES == 0:
            image_to_mate((far + [y])[k // CORES]).start()

    def text_multiply(k):
        j = order[k]

        @pl.loop(0, bc // TILE)
        def _(n):
            cols = pl.ds(pl.multiple_of(n * TILE, TILE), TILE)
            term = row_term(q_text[...], wv[j, cols, :]).astype(bf16)
            for g in range(groups):
                own_text[j, g % CORES, g // CORES, :, cols] = term[g * text_rows : (g + 1) * text_rows]

        text_to_mate(k).start()

    def add_image(yy):
        image_to_mate(yy).wait_recv()
        for t in range(shards):
            rows = piece(t)
            total = own_image[yy * CORES + core, rows].astype(f32) + mate_image[yy, rows].astype(f32)
            sum_image[yy, rows] = total.astype(bf16)
            image_to_far(yy, t).start()

    def add_text(k):
        j = order[k]
        text_to_mate(k).wait_recv()
        for yy in far:
            @pl.loop(0, text_rows // ROW_STEP)
            def _(n):
                rows = pl.ds(pl.multiple_of(n * ROW_STEP, ROW_STEP), ROW_STEP)
                total = own_text[j, core, yy, rows].astype(f32) + mate_text[j, yy, rows].astype(f32)
                sum_text[j, yy, rows] = total.astype(bf16)
            text_to_far(k, yy).start()

    lanes = lax.broadcasted_iota(jnp.int32, (span, image_rows), 1)
    slots = lax.rem(lanes, per_image)
    held = jnp.zeros((span, image_rows), jnp.int32)
    for g in range(groups):
        held = jnp.where(lanes // per_image == g, count_ref[g] * PATCH, held)
    live = slots < held

    def n_to(t):
        j = targets[t]
        return remote(n_out.at[t], nt.at[:, own_lanes], n_send.at[t], n_recv.at[me], (j, member))

    def n_from(t):
        j = targets[t]
        cols = pl.ds(pl.multiple_of(j * image_rows, image_rows), image_rows)
        return remote(n_out.at[t], nt.at[:, cols], n_send.at[t], n_recv.at[j], (j, member))

    own_lanes = pl.ds(pl.multiple_of(me * image_rows, image_rows), image_rows)

    def spread_image(t):
        if t == 0:
            image_to_mate(y).wait_recv()
        for yy in far:
            image_from_far(yy, t).wait_recv()
        rows = piece(t)
        total = own_image[member, rows].astype(f32) + mate_image[y, rows].astype(f32)
        for yy in far:
            total = total + far_image[yy, rows].astype(f32)
        total = jnp.where(live, total, 0.0).astype(bf16)
        if t < last:
            n_out[t] = total
            n_to(t).start()
        else:
            nt[:, own_lanes] = total

    for copy in q_copies[:groups]:
        copy.wait()
    for k in range(len(order)):
        image_multiply(k)
        if k % CORES == 0 and k >= CORES:
            add_image(far[k // CORES - 1])
    for copy in q_copies[groups:]:
        copy.wait()

    pending = []
    for hop in range(1, depth):
        for chunk in range(CHUNKS):
            pending.append(functools.partial(vision.relay, hop, chunk))
        for chunk in range(CHUNKS):
            pending.append(functools.partial(vision.side, hop - 1, chunk))
    for chunk in range(CHUNKS):
        pending.append(functools.partial(vision.side, depth - 1, chunk))
    images = [functools.partial(spread_image, t) for t in range(shards)]

    def step(queue, count):
        for _ in range(min(count, len(queue))):
            queue.pop(0)()

    text_multiply(0)
    step(pending, 1)
    text_multiply(1)
    step(pending, 7)
    for k in range(2, len(order)):
        add_text(k - 2)
        text_multiply(k)
        step(images, 1)
    for k in range(len(order) - 2, len(order)):
        add_text(k)
        step(images, 1)
        step(pending, 4)
    while images or pending:
        step(images, 1)
        step(pending, 2)

    gain_copy.wait()
    own_gain = gain_ref[:, pl.ds(pl.multiple_of(member * bc + me * span, span), span)]
    gain_t[...] = jnp.broadcast_to(own_gain, (image_rows, span)).T

    for t in range(last):
        w_from(t).wait_recv()

    def embed(zz):
        vision.arrive(zz)
        pair = pl.ds(pl.multiple_of(zz * SIDE * image_rows, SIDE * image_rows), SIDE * image_rows)
        rounded = row_term(wt[...], vv[pair]).astype(bf16)
        xt[:, pair] = rounded
        value = rounded.astype(f32)
        squares = jnp.sum(value * value, axis=0, keepdims=True)
        for s in range(SIDE):
            stat_own[pl.ds(zz * SIDE + s, 1)] = squares[:, s * image_rows : (s + 1) * image_rows]

    for hop in range(depth):
        vision.levels(hop, embed)

    for t in reversed(range(shards)):
        if t < last:
            n_from(t).wait_recv()
        j = targets[t]
        cols = pl.ds(pl.multiple_of(j * image_rows, image_rows), image_rows)
        scaled = gain_t[...] * nt[:, cols].astype(f32)
        inner = jnp.sum(scaled * xt[:, cols].astype(f32), axis=0, keepdims=True)
        stat_own[pl.ds(shards + j, 1)] = inner

    def stat_to(k):
        device = beside[k]
        mine = lax.rem(me, SIDE) * groups + member
        return remote(stat_own, stat_near.at[mine], s_send.at[k], s_recv.at[mine], device)

    def stat_from(k):
        device = beside[k]
        theirs = lax.rem(device[0], SIDE) * groups + device[1]
        return remote(stat_own, stat_near.at[theirs], s_send.at[k], s_recv.at[theirs], device)

    for k in range(len(beside)):
        stat_to(k).start()
    total = stat_own[...]
    for k in range(len(beside)):
        stat_from(k).wait_recv()
        total = total + stat_near[lax.rem(beside[k][0], SIDE) * groups + beside[k][1]]
    stat_sum[...] = total

    def line_to(o):
        target = lax.rem(z + o, depth)
        return remote(
            stat_sum, stat_far.at[z], z_send.at[o], z_recv.at[z], (target * SIDE + x, member)
        )

    def line_from(o):
        source = lax.rem(z + o, depth)
        return remote(
            stat_sum, stat_far.at[source], z_send.at[o], z_recv.at[source], (source * SIDE + x, member)
        )

    for o in range(1, depth):
        line_to(o).start()
    for o in range(1, depth):
        line_from(o).wait_recv()
        total = total + stat_far[lax.rem(z + o, depth)]

    inv_all = lax.rsqrt(total[:shards] / width + norm_eps)
    pull_all = inv_all**3 * (total[shards:] / width)
    for b in range(shards):
        cols = pl.ds(b * image_rows, image_rows)
        scaled = gain_t[...] * nt[:, cols].astype(f32)
        grad = inv_all[b : b + 1] * scaled - xt[:, cols].astype(f32) * pull_all[b : b + 1]
        gt[:, cols] = grad.astype(bf16)

    def o_to(t):
        j = targets[t]
        return remote(o_out.at[j], o_in.at[me], o_send.at[t], o_recv.at[me], (j, member))

    def o_from(t):
        j = targets[t]
        return remote(o_out.at[j], o_in.at[j], o_send.at[t], o_recv.at[j], (j, member))

    for i, zz in enumerate(levels):
        cols = pl.ds(pl.multiple_of(zz * SIDE * shard_k, SIDE * shard_k), SIDE * shard_k)
        out = jnp.dot(gt[...], vv[:, cols], preferred_element_type=f32) * grad_scale
        out = out.astype(bf16)
        for s in range(SIDE):
            o_out[zz * SIDE + s] = out[:, s * shard_k : (s + 1) * shard_k]
        for t in range(SIDE * i, SIDE * i + SIDE):
            if t < last:
                o_to(t).start()

    for k in range(len(order)):
        for yy in far:
            text_from_far(k, yy).wait_recv()
    t_copy.wait()

    @pl.loop(0, text_rows // ROW_STEP)
    def _(n):
        rows = pl.ds(pl.multiple_of(n * ROW_STEP, ROW_STEP), ROW_STEP)
        squares = jnp.zeros((ROW_STEP, 1), f32)
        inner = jnp.zeros((ROW_STEP, 1), f32)
        for j in range(groups):
            cols = pl.ds(j * bc, bc)
            x = tv[rows, cols].astype(f32)
            norm = own_text[j, core, y, rows].astype(f32) + mate_text[j, y, rows].astype(f32)
            for yy in far:
                norm = norm + far_text[yy, j, rows].astype(f32)
            scaled = gain_ref[:, cols] * norm
            squares += jnp.sum(x * x, axis=1, keepdims=True)
            inner += jnp.sum(x * scaled, axis=1, keepdims=True)
        inv = lax.rsqrt(squares / width + norm_eps)
        pull = inv**3 * (inner / width)
        for j in range(groups):
            cols = pl.ds(j * bc, bc)
            x = tv[rows, cols].astype(f32)
            norm = own_text[j, core, y, rows].astype(f32) + mate_text[j, y, rows].astype(f32)
            for yy in far:
                norm = norm + far_text[yy, j, rows].astype(f32)
            text_out[rows, cols] = (inv * (gain_ref[:, cols] * norm) - x * pull).astype(bf16)

    to_copy = pltpu.make_async_copy(text_out, text_hbm_out, to_sem)
    to_copy.start()

    def finish(chunk, j):
        proj_out[pl.ds(j, shard_k, stride=fold), :] = chunk.astype(f32).T

    finish(o_out[me], me)
    for t in reversed(range(last)):
        o_from(t).wait_recv()
        finish(o_in[targets[t]], targets[t])

    vision.drain()
    for t in range(last):
        w_to(t).wait_send()
        n_to(t).wait_send()
        o_to(t).wait_send()
    for k in range(len(beside)):
        stat_to(k).wait_send()
    for o in range(1, depth):
        line_to(o).wait_send()
    for k in range(len(order)):
        text_to_mate(k).wait_send()
        for yy in far:
            text_to_far(k, yy).wait_send()
    for yy in far + [y]:
        image_to_mate(yy).wait_send()
    for yy in far:
        for t in range(shards):
            image_to_far(yy, t).wait_send()
    to_copy.wait()


def place_outputs(text_in, proj_in, text_out, proj_out, text_held, proj_held, in_sem, out_sem):
    def copies(refs, sem):
        found = []
        for k, (src, dst) in enumerate(refs):
            step = src.shape[0] // PIECES
            for p in range(PIECES):
                rows = pl.ds(p * step, step)
                found.append(pltpu.make_async_copy(src.at[rows], dst.at[rows], sem.at[k, p]))
        return found

    into = copies(((text_in, text_held), (proj_in, proj_held)), in_sem)
    back = copies(((text_held, text_out), (proj_held, proj_out)), out_sem)
    for copy in into:
        copy.start()
    for first, second in zip(into, back):
        first.wait()
        second.start()
    for copy in back:
        copy.wait()


def live_rows(image_count, groups):
    image_rows = IMG_MAX * PATCH
    row_ids = jnp.arange(groups * image_rows, dtype=jnp.int32)
    owners = row_ids // image_rows
    slot_ids = row_ids % image_rows // PATCH
    owner_match = owners[:, None] == jnp.arange(groups, dtype=jnp.int32)[None, :]
    owner_counts = jnp.sum(jnp.where(owner_match, image_count[None, :], 0), axis=1)
    return (slot_ids < owner_counts)[:, None]


def fused_body(vision_rows, image_count, proj_flat, text_embeds, norm_gain, q_weight, q_grad):
    groups, shards = lax.axis_size("mp"), lax.axis_size("dp")
    model_width, bc = q_weight.shape
    image_rows, enc_width = vision_rows.shape
    text_rows = text_embeds.shape[0]
    shard_k = proj_flat.shape[0] * proj_flat.shape[1] // bc
    span = bc // shards
    chips, depth = groups // CORES, shards // SIDE
    all_rows = shards * image_rows
    grad_scale = 1.0 / float(all_rows) ** 0.5
    f32, bf16 = jnp.float32, jnp.bfloat16
    vmem, dma = pltpu.VMEM, pltpu.SemaphoreType.DMA
    on_chip = pl.BlockSpec(memory_space=pltpu.VMEM)
    scalars = pl.BlockSpec(memory_space=pltpu.SMEM)
    anywhere = pl.BlockSpec(memory_space=pl.ANY)
    text_grad, proj_block = pl.pallas_call(
        functools.partial(kernel, shards, groups, grad_scale),
        name="projector_backward",
        out_shape=(
            jax.ShapeDtypeStruct(text_embeds.shape, bf16),
            jax.ShapeDtypeStruct(proj_flat.shape, f32),
        ),
        in_specs=[scalars] + [anywhere] * 6,
        out_specs=(anywhere, on_chip),
        scratch_shapes=[
            vmem(proj_flat.shape, bf16),
            vmem((all_rows, enc_width), bf16),
            vmem((1, model_width), f32),
            vmem((image_rows, bc), bf16),
            vmem((groups * text_rows, bc), bf16),
            vmem((groups, bc, bc), bf16),
            vmem(text_embeds.shape, bf16),
            vmem(text_embeds.shape, bf16),
            vmem((groups, CORES, chips, text_rows, bc), bf16),
            vmem((groups, bc, image_rows), bf16),
            vmem((groups, chips, text_rows, bc), bf16),
            vmem((chips, bc, image_rows), bf16),
            vmem((groups, chips, text_rows, bc), bf16),
            vmem((chips, bc, image_rows), bf16),
            vmem((chips, groups, text_rows, bc), bf16),
            vmem((chips, bc, image_rows), bf16),
            vmem(proj_flat.shape, f32),
            vmem((shards, span, shard_k), bf16),
            vmem((span, enc_width), bf16),
            vmem((shards, span, image_rows), bf16),
            vmem((span, all_rows), bf16),
            vmem((span, all_rows), bf16),
            vmem((span, all_rows), bf16),
            vmem((span, image_rows), f32),
            vmem((shards, span, shard_k), bf16),
            vmem((shards, span, shard_k), bf16),
            vmem((2 * shards, image_rows), f32),
            vmem((SIDE * groups, 2 * shards, image_rows), f32),
            vmem((2 * shards, image_rows), f32),
            vmem((depth, 2 * shards, image_rows), f32),
            dma, dma, dma, dma((2, groups)), dma((groups,)), dma, dma,
            dma((3, depth, CHUNKS)), dma((shards, CHUNKS)), dma((shards, CHUNKS)), dma((shards, CHUNKS)),
            dma((shards,)), dma((shards,)), dma((shards,)), dma((shards,)), dma((shards,)), dma((shards,)),
            dma((groups,)), dma((groups,)),
            dma((chips,)), dma((chips,)),
            dma((groups, chips)), dma((chips, groups)),
            dma((chips, shards)), dma((chips, shards)),
            dma((SIDE * groups,)), dma((SIDE * groups,)),
            dma((depth,)), dma((depth,)),
        ],
        compiler_params=pltpu.CompilerParams(
            collective_id=0, has_side_effects=True, vmem_limit_bytes=56 * 1024 * 1024
        ),
    )(
        image_count,
        proj_flat,
        vision_rows,
        norm_gain[None, :],
        q_grad,
        q_weight.reshape(groups, bc, bc),
        text_embeds,
    )
    kinds = (text_grad, proj_block)
    return pl.pallas_call(
        place_outputs,
        name="place_outputs",
        out_shape=tuple(jax.ShapeDtypeStruct(a.shape, a.dtype) for a in kinds),
        in_specs=[anywhere] * 2,
        out_specs=(anywhere, anywhere),
        scratch_shapes=[vmem(a.shape, a.dtype) for a in kinds] + [dma((2, PIECES)), dma((2, PIECES))],
    )(*kinds)


def norm_back(rows_in, grads, gain):
    inputs = rows_in.astype(jnp.float32)
    inv_rms = lax.rsqrt(jnp.mean(inputs * inputs, axis=-1, keepdims=True) + norm_eps)
    scaled = gain[None, :] * grads
    inner_mean = jnp.mean(scaled * inputs, axis=-1, keepdims=True)
    return inv_rms * scaled - inputs * inv_rms**3 * inner_mean


def general_body(vision_rows, image_count, proj_flat, text_embeds, norm_gain, q_weight, q_grad):
    groups = lax.axis_size("mp")
    member = lax.axis_index("mp")
    shards = lax.axis_size("dp")
    enc_width = vision_rows.shape[1]
    block_cols = q_weight.shape[1]
    model_width = q_weight.shape[0]
    used_count = enc_width * block_cols
    image_rows = IMG_MAX * PATCH
    gathered = lax.all_gather(proj_flat, "dp", axis=0, tiled=True)
    proj_block = gathered.reshape(-1)[:used_count].reshape(enc_width, block_cols)
    embed_cols = jnp.dot(vision_rows, proj_block, preferred_element_type=jnp.float32).astype(
        jnp.bfloat16
    )
    live_group = live_rows(image_count, groups)
    blocks = q_grad.reshape(groups, ROWS_DEV, block_cols)
    image_query = blocks[:, :image_rows].reshape(-1, block_cols)
    text_query = blocks[:, image_rows:].reshape(-1, block_cols)
    image_term = row_term(image_query, q_weight)
    image_norm = lax.psum_scatter(
        image_term.astype(jnp.bfloat16), "mp", scatter_dimension=1, tiled=True
    ).astype(jnp.float32)
    text_norm = lax.psum_scatter(
        row_term(text_query, q_weight).astype(jnp.bfloat16), "mp", scatter_dimension=0, tiled=True
    ).astype(jnp.float32)
    x_cols = embed_cols.astype(jnp.float32)
    gain_cols = lax.dynamic_slice_in_dim(norm_gain, member * block_cols, block_cols)
    scaled = gain_cols[None, :] * image_norm
    squares, inner_sum = lax.psum(
        (jnp.sum(x_cols * x_cols, axis=1), jnp.sum(scaled * x_cols, axis=1)), "mp"
    )
    inv_rms = lax.rsqrt(squares / model_width + norm_eps)[:, None]
    image_input = inv_rms * scaled - x_cols * inv_rms**3 * (inner_sum / model_width)[:, None]
    image_cols = jnp.where(live_group, image_input, 0.0).astype(jnp.bfloat16)
    text_grad = norm_back(text_embeds, text_norm, norm_gain).astype(jnp.bfloat16)
    grad_scale = 1.0 / jnp.sqrt(jnp.float32(shards * groups * image_rows))
    proj_part = (
        lax.dot_general(
            vision_rows, image_cols, (((0,), (0,)), ((), ())), preferred_element_type=jnp.float32
        )
        * grad_scale
    )
    stored_rows = proj_flat.shape[0]
    padded = jnp.pad(proj_part.reshape(-1), (0, shards * stored_rows * 128 - used_count))
    padded = padded.reshape(shards * stored_rows, 128)
    proj_grad = lax.psum_scatter(padded, "dp", scatter_dimension=0, tiled=True)
    return (text_grad, proj_grad)


def body(vision_rows, image_count, proj_flat, text_embeds, norm_gain, q_weight, q_grad):
    groups, shards = lax.axis_size("mp"), lax.axis_size("dp")
    bc = q_weight.shape[1]
    count = proj_flat.shape[0] * proj_flat.shape[1]
    shard_k = count // bc
    fits = (
        count % bc == 0
        and shard_k == LANES
        and bc == shards * LANES
        and shard_k * shards == vision_rows.shape[1]
        and shard_k == vision_rows.shape[0]
        and bc % TILE == 0
        and groups > CORES
        and groups % CORES == 0
        and vision_rows.shape[0] // groups % ROW_STEP == 0
        and text_embeds.shape[0] % (PIECES * ROW_STEP) == 0
        and shards > SIDE
        and shards % SIDE == 0
    )
    run = fused_body if fits else general_body
    return run(vision_rows, image_count, proj_flat, text_embeds, norm_gain, q_weight, q_grad)


def solution(mesh):
    return jax.shard_map(
        body,
        mesh=mesh,
        in_specs=(
            P("dp", None),
            P("dp"),
            P(("dp", "mp"), None),
            P(("dp", "mp"), None),
            P(),
            P(None, "mp"),
            P("dp", "mp"),
        ),
        out_specs=(P(("dp", "mp"), None), P(("dp", "mp"), None)),
        check_vma=False,
    )
```

time: 62.9 us -> 53.5 us (0.85)
  Pallas kernels: 62.1 us -> 52.7 us
    pallas_call x1, Pallas kernels: 60 us -> 50.6 us  [fused_body(): pl.pallas_call(functools.partial(kernel, shards, groups, grad_scale), nam...]
where the time goes in v1:
time: 53.5 us; the launch traced here: 53.4 us
  Pallas kernels  52.7 us (99%)
  between operations  0.64 us (1%)
    pallas_call x1, Pallas kernels, fused_body(): pl.pallas_call(functools.partial(kernel, shards, groups, grad_scale), nam...  50.6 us
    pallas_call x1, Pallas kernels, fused_body(): pl.pallas_call(place_outputs, name='place_outputs', out_shape=tuple((jax....  2.11 us

profile of v1, /device:TPU:0, one launch (start us, length us, event | category | flops | bytes accessed | tf_op | source)
XLA Modules:
  0.0 53.4 jit_solution(4918063530388033226)
XLA Ops:
  0.6 50.6 %projector_backward.1 = (bf16[96,4096]{1,0:T(8,128)(2,1)}, f32[1024,128]{1,0:T(8,128)}) custom-call(s32[4]{0:T(128)} %count_ref.1, bf16[1024,128]{1,0:T(8,128)(2,1)} %proj_hbm.1, bf16[128,1024]{1,0:T(8,128)(2,1)} %vision_hbm.1, f32[1,4096]{1,0:T(1,128)} %bitcast.3, bf16[512,1024]{1,0:T(8,128)(2,1)} %q_hbm.1, bf16[4,1024,1024]{2,1,0:T(8,128)(2,1)} %bitcast.2, ...), custom_call_target="tpu_custom_call" | custom-call | tf_op jit(solution)/shard_map/projector_backward/pallas_call | solution.py:607
  51.2 2.1 %place_outputs.1 = (bf16[96,4096]{1,0:T(8,128)(2,1)}, f32[1024,128]{1,0:T(8,128)}) custom-call(bf16[96,4096]{1,0:T(8,128)(2,1)} %get-tuple-element.4.text_in, f32[1024,128]{1,0:T(8,128)} %get-tuple-element.5.proj_in), custom_call_target="tpu_custom_call" | custom-call | tf_op jit(solution)/shard_map/place_outputs/pallas_call | solution.py:670

commit v2 on v1

--- a/solution.py
+++ b/solution.py
@@ -15,7 +15,6 @@
 CHUNKS = 4
 PIECES = 2
 LANES = 128
-TILE = 256
 ROW_STEP = 16
 
 MESH = pl.DeviceIdType.MESH
@@ -57,23 +56,25 @@
         place = self.place(block, chunk, self.core)
         target = (self.me + SIDE, self.me - SIDE, self.z * SIDE + 1 - self.x)[way]
         return remote(
-            place, place, self.send.at[way, zz, chunk], self.recv.at[block, chunk],
+            place, place, self.send.at[way], self.recv.at[block, chunk],
             (target, self.member),
         )
 
     def to_mate(self, block, chunk):
         place = self.place(block, chunk, self.core)
         return remote(
-            place, place, self.mate_send.at[block, chunk], self.mate_recv.at[block, chunk],
+            place, place, self.mate_send, self.mate_recv.at[block],
             (self.me, self.mate),
         )
 
-    def from_mate(self, block, chunk):
-        place = self.place(block, chunk, 1 - self.core)
-        return remote(
-            place, place, self.mate_send.at[block, chunk], self.mate_recv.at[block, chunk],
-            (self.me, self.mate),
-        )
+    def from_mate(self, block):
+        first = block * self.block_rows + (1 - self.core) * self.half
+        place = self.buf.at[pl.ds(pl.multiple_of(first, self.half), self.half)]
+        return remote(place, place, self.mate_send, self.mate_recv.at[block], (self.me, self.mate))
+
+    def sent(self, send, blocks):
+        place = self.buf.at[pl.ds(0, blocks * self.half)]
+        remote(place, place, send, self.mate_recv.at[0], (self.me, self.mate)).wait_send()
 
     def start(self):
         for chunk in range(CHUNKS):
@@ -126,45 +127,36 @@
         self.levels(hop, take)
 
     def arrive(self, zz):
-        for chunk in range(CHUNKS):
-            @pl.when(zz != self.z)
-            def _():
-                self.from_mate(zz * SIDE + self.x, chunk).wait_recv()
-
-            self.from_mate(zz * SIDE + 1 - self.x, chunk).wait_recv()
+        @pl.when(zz != self.z)
+        def _():
+            self.from_mate(zz * SIDE + self.x).wait_recv()
+
+        self.from_mate(zz * SIDE + 1 - self.x).wait_recv()
 
     def drain(self):
         for zz in range(self.depth):
-            for chunk in range(CHUNKS):
-                @pl.when((self.z >= zz) & (self.z < self.depth - 1))
-                def _():
-                    self.copy(zz, self.x, chunk, 0).wait_send()
-
-                @pl.when((self.z <= zz) & (self.z > 0))
-                def _():
-                    self.copy(zz, self.x, chunk, 1).wait_send()
-
-                self.copy(zz, self.x, chunk, 2).wait_send()
-
-                @pl.when(zz != self.z)
-                def _():
-                    self.to_mate(zz * SIDE + self.x, chunk).wait_send()
-
-                self.to_mate(zz * SIDE + 1 - self.x, chunk).wait_send()
+            @pl.when(self.z == zz)
+            def _():
+                if zz < self.depth - 1:
+                    self.sent(self.send.at[0], zz + 1)
+                if zz > 0:
+                    self.sent(self.send.at[1], self.depth - zz)
+        self.sent(self.send.at[2], self.depth)
+        self.sent(self.mate_send, SIDE * self.depth - 1)
 
 
 def kernel(
     shards, groups, grad_scale,
     count_ref, proj_hbm, vision_hbm, gain_hbm, q_hbm, w_hbm, text_hbm,
-    text_hbm_out, proj_out,
-    pv, vv, gain_ref, q_image, q_text, wv, tv, text_out,
+    text_out, proj_out,
+    pv, vv, gain_ref, q_image, q_text, wv, tv,
     own_text, own_image, mate_text, mate_image, sum_text, sum_image,
     far_text, far_image, w_flat, w_out, wt, n_out, nt, xt, gt, gain_t, o_out, o_in,
-    stat_own, stat_near, stat_sum, stat_far,
-    p_sem, vis_sem, gain_sem, q_sem, w_sem, t_sem, to_sem,
+    stat_f32, stat_own, stat_near, stat_sum, stat_far,
+    p_sem, vis_sem, gain_sem, q_sem, w_sem, t_sem,
     v_send, v_recv, vm_send, vm_recv, wt_send, wt_recv, n_send, n_recv, o_send, o_recv,
     mt_send, mt_recv, mi_send, mi_recv, ft_send, ft_recv, fi_send, fi_recv,
-    s_send, s_recv, z_send, z_recv,
+    s_send, s_recv, z_send, z_recv, up_sem, down_sem,
 ):
     me, member = lax.axis_index("dp"), lax.axis_index("mp")
     depth = shards // SIDE
@@ -190,7 +182,6 @@
     targets = [
         lax.rem(z + o, depth) * SIDE + (x if flip else 1 - x) for o in offsets for flip in (0, 1)
     ]
-    levels = [lax.rem(z + o, depth) for o in offsets]
     last = shards - 1
 
     p_copy = pltpu.make_async_copy(proj_hbm, pv, p_sem)
@@ -198,81 +189,96 @@
     own_rows = pl.ds(pl.multiple_of(me * image_rows, image_rows), image_rows)
     vis_copy = pltpu.make_async_copy(vision_hbm, vv.at[own_rows], vis_sem)
     vis_copy.start()
-    q_copies = []
-    for g in range(groups):
-        q_copies.append(pltpu.make_async_copy(
-            q_hbm.at[pl.ds(g * rows_dev, per_image)],
-            q_image.at[pl.ds(g * per_image, per_image)], q_sem.at[0, g],
-        ))
-    for g in range(groups):
-        q_copies.append(pltpu.make_async_copy(
-            q_hbm.at[pl.ds(g * rows_dev + per_image, text_rows)],
-            q_text.at[pl.ds(g * text_rows, text_rows)], q_sem.at[1, g],
-        ))
+    q_copies = [
+        pltpu.make_async_copy(
+            q_hbm.at[pl.ds(g * rows_dev + first, count)], dst.at[pl.ds(g * count, count)], q_sem.at[k]
+        )
+        for k, (first, count, dst) in enumerate(((0, per_image, q_image), (per_image, text_rows, q_text)))
+        for g in range(groups)
+    ]
+    q_image_done = pltpu.make_async_copy(q_hbm.at[pl.ds(0, image_rows)], q_image, q_sem.at[0])
+    q_text_done = pltpu.make_async_copy(q_hbm.at[pl.ds(0, groups * text_rows)], q_text, q_sem.at[1])
     w_copies = [pltpu.make_async_copy(w_hbm.at[j], wv.at[j], w_sem.at[k]) for k, j in enumerate(order)]
-    for copy in q_copies[:groups] + w_copies[:1] + q_copies[groups:] + w_copies[1:]:
+    gain_copy = pltpu.make_async_copy(gain_hbm, gain_ref, gain_sem)
+    t_copy = pltpu.make_async_copy(text_hbm, tv, t_sem)
+    for copy in q_copies[:groups] + w_copies[:1]:
         copy.start()
-    gain_copy = pltpu.make_async_copy(gain_hbm, gain_ref, gain_sem)
-    gain_copy.start()
-    t_copy = pltpu.make_async_copy(text_hbm, tv, t_sem)
-    t_copy.start()
 
     barrier = pltpu.get_barrier_semaphore()
     across = z * SIDE + 1 - x
     beside = [(me, lax.rem(member + step, groups)) for step in range(1, groups)]
     beside += [(across, lax.rem(member + step, groups)) for step in range(groups)]
-    peers = [(lax.rem(me + SIDE * o, shards), member) for o in range(1, depth)]
-    peers += [(lax.rem(across + SIDE * o, shards), member) for o in range(1, depth)]
-    for device in beside + peers:
+    for device in beside:
         pl.semaphore_signal(barrier, inc=1, device_id=device, device_id_type=MESH)
+
+    @pl.when(z > 0)
+    def _():
+        pl.semaphore_signal(barrier, inc=1, device_id=(me - SIDE, member), device_id_type=MESH)
+
+    @pl.when(z < depth - 1)
+    def _():
+        pl.semaphore_signal(barrier, inc=1, device_id=(me + SIDE, member), device_id_type=MESH)
+
+    def pass_on(hop):
+        @pl.when(z == hop)
+        def _():
+            if hop > 0:
+                pl.semaphore_wait(up_sem, 1)
+            if hop < depth - 1:
+                pl.semaphore_signal(up_sem, inc=1, device_id=(me + SIDE, member), device_id_type=MESH)
+
+        @pl.when(depth - 1 - z == hop)
+        def _():
+            if hop > 0:
+                pl.semaphore_wait(down_sem, 1)
+            if hop < depth - 1:
+                pl.semaphore_signal(down_sem, inc=1, device_id=(me - SIDE, member), device_id_type=MESH)
+
+    vis_copy.wait()
+    for copy in w_copies[1:] + q_copies[groups:] + [gain_copy, t_copy]:
+        copy.start()
+
+    @pl.when((z == 0) | (z == depth - 1))
+    def _():
+        pl.semaphore_wait(barrier, len(beside) + 1)
+
+    @pl.when((z > 0) & (z < depth - 1))
+    def _():
+        pl.semaphore_wait(barrier, len(beside) + 2)
+
+    vision = VisionGather(depth, me, member, vv, image_rows, v_send, v_recv, vm_send, vm_recv)
+    vision.start()
+    pass_on(0)
 
     p_copy.wait()
     w_flat[...] = pv[...].astype(f32)
     for j in range(shards):
-        w_out[j] = w_flat[pl.ds(j, shard_k, stride=fold), :].T.astype(bf16)
+        w_out[j] = w_flat[pl.ds(j, shard_k, stride=fold), :].astype(bf16).T
     own_k = pl.ds(pl.multiple_of(me * shard_k, shard_k), shard_k)
     wt[:, own_k] = w_out[me]
-    vis_copy.wait()
-
-    pl.semaphore_wait(barrier, len(beside) + len(peers))
-
-    vision = VisionGather(depth, me, member, vv, image_rows, v_send, v_recv, vm_send, vm_recv)
-    vision.start()
 
     def w_to(t):
         j = targets[t]
-        return remote(w_out.at[j], wt.at[:, own_k], wt_send.at[t], wt_recv.at[me], (j, member))
-
-    def w_from(t):
-        j = targets[t]
-        cols = pl.ds(pl.multiple_of(j * shard_k, shard_k), shard_k)
-        return remote(w_out.at[j], wt.at[:, cols], wt_send.at[t], wt_recv.at[j], (j, member))
-
-    for t in range(last):
-        w_to(t).start()
+        return remote(w_out.at[j], wt.at[:, own_k], wt_send, wt_recv, (j, member))
+
+    def all_to(buf, send, recv):
+        place = buf.at[pl.ds(0, last)]
+        return remote(place, place, send, recv, (me, mate))
 
     def text_to_mate(k):
         j = order[k]
-        return remote(own_text.at[j, 1 - core], mate_text.at[j], mt_send.at[j], mt_recv.at[j], (me, mate))
+        return remote(own_text.at[j, 1 - core], mate_text.at[j], mt_send, mt_recv.at[j], (me, mate))
 
     def image_to_mate(yy):
         return remote(
             own_image.at[yy * CORES + 1 - core], mate_image.at[yy],
-            mi_send.at[yy], mi_recv.at[yy], (me, mate),
+            mi_send, mi_recv.at[yy], (me, mate),
         )
 
     def text_to_far(k, yy):
         j = order[k]
         return remote(
-            sum_text.at[j, yy], far_text.at[y, j], ft_send.at[j, yy], ft_recv.at[y, j],
-            (me, yy * CORES + core),
-        )
-
-    def text_from_far(k, yy):
-        j = order[k]
-        return remote(
-            sum_text.at[j, yy], far_text.at[yy, j], ft_send.at[j, yy], ft_recv.at[yy, j],
-            (me, yy * CORES + core),
+            sum_text.at[j, yy], far_text.at[y, j], ft_send, ft_recv, (me, yy * CORES + core)
         )
 
     def piece(t):
@@ -281,22 +287,22 @@
     def image_to_far(yy, t):
         return remote(
             sum_image.at[yy, piece(t)], far_image.at[y, piece(t)],
-            fi_send.at[yy, t], fi_recv.at[y, t], (me, yy * CORES + core),
+            fi_send, fi_recv.at[y, t], (me, yy * CORES + core),
         )
 
     def image_from_far(yy, t):
         return remote(
             sum_image.at[yy, piece(t)], far_image.at[yy, piece(t)],
-            fi_send.at[yy, t], fi_recv.at[yy, t], (me, yy * CORES + core),
+            fi_send, fi_recv.at[yy, t], (me, yy * CORES + core),
         )
 
     def image_multiply(k):
         j = order[k]
         w_copies[k].wait()
 
-        @pl.loop(0, bc // TILE)
+        @pl.loop(0, 1)
         def _(n):
-            rows = pl.ds(pl.multiple_of(n * TILE, TILE), TILE)
+            rows = pl.ds(pl.multiple_of(n * bc, bc), bc)
             own_image[j, rows] = row_term(wv[j, rows], q_image[...]).astype(bf16)
 
         if k % CORES == 0:
@@ -304,14 +310,9 @@
 
     def text_multiply(k):
         j = order[k]
-
-        @pl.loop(0, bc // TILE)
-        def _(n):
-            cols = pl.ds(pl.multiple_of(n * TILE, TILE), TILE)
-            term = row_term(q_text[...], wv[j, cols, :]).astype(bf16)
-            for g in range(groups):
-                own_text[j, g % CORES, g // CORES, :, cols] = term[g * text_rows : (g + 1) * text_rows]
-
+        term = row_term(q_text[...], wv[j]).astype(bf16)
+        for g in range(groups):
+            own_text[j, g % CORES, g // CORES] = term[g * text_rows : (g + 1) * text_rows]
         text_to_mate(k).start()
 
     def add_image(yy):
@@ -342,12 +343,7 @@
 
     def n_to(t):
         j = targets[t]
-        return remote(n_out.at[t], nt.at[:, own_lanes], n_send.at[t], n_recv.at[me], (j, member))
-
-    def n_from(t):
-        j = targets[t]
-        cols = pl.ds(pl.multiple_of(j * image_rows, image_rows), image_rows)
-        return remote(n_out.at[t], nt.at[:, cols], n_send.at[t], n_recv.at[j], (j, member))
+        return remote(n_out.at[t], nt.at[:, own_lanes], n_send, n_recv, (j, member))
 
     own_lanes = pl.ds(pl.multiple_of(me * image_rows, image_rows), image_rows)
 
@@ -367,51 +363,52 @@
         else:
             nt[:, own_lanes] = total
 
-    for copy in q_copies[:groups]:
-        copy.wait()
+    def each(action, *lead):
+        return [functools.partial(action, *lead, chunk) for chunk in range(CHUNKS)]
+
+    def play(*actions):
+        for action in actions:
+            action()
+
+    images = [functools.partial(spread_image, t) for t in range(shards)]
+
+    first, rest = each(vision.relay, 1)[:2], each(vision.relay, 1)[2:]
+    q_image_done.wait()
     for k in range(len(order)):
         image_multiply(k)
+        if k + 1 < depth - 1:
+            pass_on(k + 1)
         if k % CORES == 0 and k >= CORES:
             add_image(far[k // CORES - 1])
-    for copy in q_copies[groups:]:
-        copy.wait()
-
-    pending = []
-    for hop in range(1, depth):
-        for chunk in range(CHUNKS):
-            pending.append(functools.partial(vision.relay, hop, chunk))
-        for chunk in range(CHUNKS):
-            pending.append(functools.partial(vision.side, hop - 1, chunk))
-    for chunk in range(CHUNKS):
-        pending.append(functools.partial(vision.side, depth - 1, chunk))
-    images = [functools.partial(spread_image, t) for t in range(shards)]
-
-    def step(queue, count):
-        for _ in range(min(count, len(queue))):
-            queue.pop(0)()
-
+            if k == CORES:
+                play(*first)
+    for hop in range(min(len(order) + 1, depth - 1), depth):
+        pass_on(hop)
+    play(*rest)
+    for t in range(last):
+        w_to(t).start()
+    q_text_done.wait()
     text_multiply(0)
-    step(pending, 1)
+    play(*each(vision.side, 0))
+    play(*images[:1])
     text_multiply(1)
-    step(pending, 7)
+    play(*images[1:2])
+    add_text(0)
+    waves = [each(vision.relay, hop) for hop in range(2, depth)]
+    flow = [action for wave in waves for action in wave]
     for k in range(2, len(order)):
-        add_text(k - 2)
         text_multiply(k)
-        step(images, 1)
-    for k in range(len(order) - 2, len(order)):
-        add_text(k)
-        step(images, 1)
-        step(pending, 4)
-    while images or pending:
-        step(images, 1)
-        step(pending, 2)
-
+        play(*images[2 * k - 2 : 2 * k])
+        play(*flow[2 * k - 4 : 2 * k - 2])
+        if k == 2:
+            add_text(1)
+    play(*images[2 * len(order) - 2 :])
     gain_copy.wait()
     own_gain = gain_ref[:, pl.ds(pl.multiple_of(member * bc + me * span, span), span)]
     gain_t[...] = jnp.broadcast_to(own_gain, (image_rows, span)).T
-
-    for t in range(last):
-        w_from(t).wait_recv()
+    play(*each(vision.side, 1))
+    play(*flow[2 * len(order) - 4 :])
+    all_to(w_out, wt_send, wt_recv).wait_recv()
 
     def embed(zz):
         vision.arrive(zz)
@@ -421,55 +418,55 @@
         value = rounded.astype(f32)
         squares = jnp.sum(value * value, axis=0, keepdims=True)
         for s in range(SIDE):
-            stat_own[pl.ds(zz * SIDE + s, 1)] = squares[:, s * image_rows : (s + 1) * image_rows]
+            stat_f32[pl.ds(zz * SIDE + s, 1)] = squares[:, s * image_rows : (s + 1) * image_rows]
 
     for hop in range(depth):
-        vision.levels(hop, embed)
-
-    for t in reversed(range(shards)):
-        if t < last:
-            n_from(t).wait_recv()
-        j = targets[t]
-        cols = pl.ds(pl.multiple_of(j * image_rows, image_rows), image_rows)
+        if hop >= 2:
+            play(*each(vision.side, hop))
+        if hop < depth - 1:
+            vision.levels(hop, embed)
+    vision.levels(depth - 1, embed)
+
+    all_to(n_out, n_send, n_recv).wait_recv()
+    for j in range(shards):
+        cols = pl.ds(j * image_rows, image_rows)
         scaled = gain_t[...] * nt[:, cols].astype(f32)
         inner = jnp.sum(scaled * xt[:, cols].astype(f32), axis=0, keepdims=True)
-        stat_own[pl.ds(shards + j, 1)] = inner
+        stat_f32[pl.ds(shards + j, 1)] = inner
+    stat_own[...] = stat_f32[...].astype(bf16)
 
     def stat_to(k):
         device = beside[k]
         mine = lax.rem(me, SIDE) * groups + member
-        return remote(stat_own, stat_near.at[mine], s_send.at[k], s_recv.at[mine], device)
-
-    def stat_from(k):
-        device = beside[k]
-        theirs = lax.rem(device[0], SIDE) * groups + device[1]
-        return remote(stat_own, stat_near.at[theirs], s_send.at[k], s_recv.at[theirs], device)
-
+        return remote(stat_own, stat_near.at[mine], s_send, s_recv, device)
+
+    near_done = pl.ds(0, len(beside))
+    stat_near_done = remote(
+        stat_near.at[near_done], stat_near.at[near_done], s_send, s_recv, (me, mate)
+    )
     for k in range(len(beside)):
         stat_to(k).start()
-    total = stat_own[...]
-    for k in range(len(beside)):
-        stat_from(k).wait_recv()
-        total = total + stat_near[lax.rem(beside[k][0], SIDE) * groups + beside[k][1]]
-    stat_sum[...] = total
+    for k in range(2, len(order)):
+        add_text(k)
+    total = stat_f32[...]
+    stat_near_done.wait_recv()
+    for device in beside:
+        total = total + stat_near[lax.rem(device[0], SIDE) * groups + device[1]].astype(f32)
+    stat_sum[...] = total.astype(bf16)
 
     def line_to(o):
         target = lax.rem(z + o, depth)
-        return remote(
-            stat_sum, stat_far.at[z], z_send.at[o], z_recv.at[z], (target * SIDE + x, member)
-        )
-
-    def line_from(o):
-        source = lax.rem(z + o, depth)
-        return remote(
-            stat_sum, stat_far.at[source], z_send.at[o], z_recv.at[source], (source * SIDE + x, member)
-        )
-
+        return remote(stat_sum, stat_far.at[z], z_send, z_recv, (target * SIDE + x, member))
+
+    far_done = pl.ds(0, depth - 1)
+    stat_far_done = remote(
+        stat_far.at[far_done], stat_far.at[far_done], z_send, z_recv, (me, mate)
+    )
     for o in range(1, depth):
         line_to(o).start()
+    stat_far_done.wait_recv()
     for o in range(1, depth):
-        line_from(o).wait_recv()
-        total = total + stat_far[lax.rem(z + o, depth)]
+        total = total + stat_far[lax.rem(z + o, depth)].astype(f32)
 
     inv_all = lax.rsqrt(total[:shards] / width + norm_eps)
     pull_all = inv_all**3 * (total[shards:] / width)
@@ -481,25 +478,21 @@
 
     def o_to(t):
         j = targets[t]
-        return remote(o_out.at[j], o_in.at[me], o_send.at[t], o_recv.at[me], (j, member))
+        return remote(o_out.at[j], o_in.at[me], o_send, o_recv.at[me], (j, member))
 
     def o_from(t):
         j = targets[t]
-        return remote(o_out.at[j], o_in.at[j], o_send.at[t], o_recv.at[j], (j, member))
-
-    for i, zz in enumerate(levels):
-        cols = pl.ds(pl.multiple_of(zz * SIDE * shard_k, SIDE * shard_k), SIDE * shard_k)
-        out = jnp.dot(gt[...], vv[:, cols], preferred_element_type=f32) * grad_scale
-        out = out.astype(bf16)
-        for s in range(SIDE):
-            o_out[zz * SIDE + s] = out[:, s * shard_k : (s + 1) * shard_k]
-        for t in range(SIDE * i, SIDE * i + SIDE):
-            if t < last:
-                o_to(t).start()
-
-    for k in range(len(order)):
-        for yy in far:
-            text_from_far(k, yy).wait_recv()
+        return remote(o_out.at[j], o_in.at[j], o_send, o_recv.at[j], (j, member))
+
+    out = (jnp.dot(gt[...], vv[...], preferred_element_type=f32) * grad_scale).astype(bf16)
+    for j in range(shards):
+        o_out[j] = out[:, j * shard_k : (j + 1) * shard_k]
+    for t in range(last):
+        o_to(t).start()
+
+    text_far = sum_text.at[:, pl.ds(0, len(far))]
+    text_far_done = remote(text_far, text_far, ft_send, ft_recv, (me, mate))
+    text_far_done.wait_recv()
     t_copy.wait()
 
     @pl.loop(0, text_rows // ROW_STEP)
@@ -526,9 +519,6 @@
                 norm = norm + far_text[yy, j, rows].astype(f32)
             text_out[rows, cols] = (inv * (gain_ref[:, cols] * norm) - x * pull).astype(bf16)
 
-    to_copy = pltpu.make_async_copy(text_out, text_hbm_out, to_sem)
-    to_copy.start()
-
     def finish(chunk, j):
         proj_out[pl.ds(j, shard_k, stride=fold), :] = chunk.astype(f32).T
 
@@ -538,44 +528,28 @@
         finish(o_in[targets[t]], targets[t])
 
     vision.drain()
-    for t in range(last):
-        w_to(t).wait_send()
-        n_to(t).wait_send()
-        o_to(t).wait_send()
-    for k in range(len(beside)):
-        stat_to(k).wait_send()
-    for o in range(1, depth):
-        line_to(o).wait_send()
-    for k in range(len(order)):
-        text_to_mate(k).wait_send()
-        for yy in far:
-            text_to_far(k, yy).wait_send()
-    for yy in far + [y]:
-        image_to_mate(yy).wait_send()
-    for yy in far:
-        for t in range(shards):
-            image_to_far(yy, t).wait_send()
-    to_copy.wait()
-
-
-def place_outputs(text_in, proj_in, text_out, proj_out, text_held, proj_held, in_sem, out_sem):
-    def copies(refs, sem):
-        found = []
-        for k, (src, dst) in enumerate(refs):
-            step = src.shape[0] // PIECES
-            for p in range(PIECES):
-                rows = pl.ds(p * step, step)
-                found.append(pltpu.make_async_copy(src.at[rows], dst.at[rows], sem.at[k, p]))
-        return found
-
-    into = copies(((text_in, text_held), (proj_in, proj_held)), in_sem)
-    back = copies(((text_held, text_out), (proj_held, proj_out)), out_sem)
-    for copy in into:
+    all_to(w_out, wt_send, wt_recv).wait_send()
+    all_to(n_out, n_send, n_recv).wait_send()
+    all_to(o_out, o_send, o_recv.at[0]).wait_send()
+    stat_near_done.wait_send()
+    stat_far_done.wait_send()
+    text_far_done.wait_send()
+    remote(mate_text, mate_text, mt_send, mt_recv.at[0], (me, mate)).wait_send()
+    remote(mate_image, mate_image, mi_send, mi_recv.at[0], (me, mate)).wait_send()
+    image_far = sum_image.at[pl.ds(0, len(far))]
+    remote(image_far, image_far, fi_send, fi_recv.at[0, 0], (me, mate)).wait_send()
+
+
+def place_outputs(text_in, proj_in, text_out, proj_out, sem):
+    copies = []
+    for k, (src, dst) in enumerate(((text_in, text_out), (proj_in, proj_out))):
+        step = src.shape[0] // PIECES
+        for p in range(PIECES):
+            rows = pl.ds(p * step, step)
+            copies.append(pltpu.make_async_copy(src.at[rows], dst.at[rows], sem.at[k, p]))
+    for copy in copies:
         copy.start()
-    for first, second in zip(into, back):
-        first.wait()
-        second.start()
-    for copy in back:
+    for copy in copies:
         copy.wait()
 
 
@@ -603,16 +577,13 @@
     vmem, dma = pltpu.VMEM, pltpu.SemaphoreType.DMA
     on_chip = pl.BlockSpec(memory_space=pltpu.VMEM)
     scalars = pl.BlockSpec(memory_space=pltpu.SMEM)
-    anywhere = pl.BlockSpec(memory_space=pl.ANY)
+    in_hbm = pl.BlockSpec(memory_space=pltpu.HBM)
     text_grad, proj_block = pl.pallas_call(
         functools.partial(kernel, shards, groups, grad_scale),
         name="projector_backward",
-        out_shape=(
-            jax.ShapeDtypeStruct(text_embeds.shape, bf16),
-            jax.ShapeDtypeStruct(proj_flat.shape, f32),
-        ),
-        in_specs=[scalars] + [anywhere] * 6,
-        out_specs=(anywhere, on_chip),
+        out_shape=(vmem(text_embeds.shape, bf16), vmem(proj_flat.shape, f32)),
+        in_specs=[scalars] + [in_hbm] * 6,
+        out_specs=(on_chip, on_chip),
         scratch_shapes=[
             vmem(proj_flat.shape, bf16),
             vmem((all_rows, enc_width), bf16),
@@ -620,7 +591,6 @@
             vmem((image_rows, bc), bf16),
             vmem((groups * text_rows, bc), bf16),
             vmem((groups, bc, bc), bf16),
-            vmem(text_embeds.shape, bf16),
             vmem(text_embeds.shape, bf16),
             vmem((groups, CORES, chips, text_rows, bc), bf16),
             vmem((groups, bc, image_rows), bf16),
@@ -641,18 +611,15 @@
             vmem((shards, span, shard_k), bf16),
             vmem((shards, span, shard_k), bf16),
             vmem((2 * shards, image_rows), f32),
-            vmem((SIDE * groups, 2 * shards, image_rows), f32),
-            vmem((2 * shards, image_rows), f32),
-            vmem((depth, 2 * shards, image_rows), f32),
-            dma, dma, dma, dma((2, groups)), dma((groups,)), dma, dma,
-            dma((3, depth, CHUNKS)), dma((shards, CHUNKS)), dma((shards, CHUNKS)), dma((shards, CHUNKS)),
-            dma((shards,)), dma((shards,)), dma((shards,)), dma((shards,)), dma((shards,)), dma((shards,)),
-            dma((groups,)), dma((groups,)),
-            dma((chips,)), dma((chips,)),
-            dma((groups, chips)), dma((chips, groups)),
-            dma((chips, shards)), dma((chips, shards)),
-            dma((SIDE * groups,)), dma((SIDE * groups,)),
-            dma((depth,)), dma((depth,)),
+            vmem((2 * shards, image_rows), bf16),
+            vmem((SIDE * groups, 2 * shards, image_rows), bf16),
+            vmem((2 * shards, image_rows), bf16),
+            vmem((depth, 2 * shards, image_rows), bf16),
+            dma, dma, dma, dma((2,)), dma((groups,)), dma,
+            dma((3,)), dma((shards, CHUNKS)), dma, dma((shards,)),
+            dma, dma, dma, dma, dma, dma((shards,)),
+            dma, dma((groups,)), dma, dma((chips,)), dma, dma, dma, dma((chips, shards)),
+            dma, dma, dma, dma, pltpu.SemaphoreType.REGULAR, pltpu.SemaphoreType.REGULAR,
         ],
         compiler_params=pltpu.CompilerParams(
             collective_id=0, has_side_effects=True, vmem_limit_bytes=56 * 1024 * 1024
@@ -671,9 +638,10 @@
         place_outputs,
         name="place_outputs",
         out_shape=tuple(jax.ShapeDtypeStruct(a.shape, a.dtype) for a in kinds),
-        in_specs=[anywhere] * 2,
-        out_specs=(anywhere, anywhere),
-        scratch_shapes=[vmem(a.shape, a.dtype) for a in kinds] + [dma((2, PIECES)), dma((2, PIECES))],
+        in_specs=[on_chip] * 2,
+        out_specs=(in_hbm, in_hbm),
+        scratch_shapes=[dma((2, PIECES))],
+        compiler_params=pltpu.CompilerParams(vmem_limit_bytes=4 * 1024 * 1024),
     )(*kinds)
 
 
@@ -745,7 +713,6 @@
         and bc == shards * LANES
         and shard_k * shards == vision_rows.shape[1]
         and shard_k == vision_rows.shape[0]
-        and bc % TILE == 0
         and groups > CORES
         and groups % CORES == 0
         and vision_rows.shape[0] // groups % ROW_STEP == 0

time: 53.5 us -> 46.1 us (0.86)
  Pallas kernels: 52.7 us -> 45.3 us
    pallas_call x1, Pallas kernels: 50.6 us -> 44.2 us  [fused_body(): pl.pallas_call(functools.partial(kernel, shards, groups, grad_scale), nam...]
    pallas_call x1, Pallas kernels: 2.11 us -> 1.09 us  [fused_body(): pl.pallas_call(place_outputs, name='place_outputs', out_shape=tuple((jax....]
where the time goes in v2:
time: 46.1 us; the launch traced here: 46 us
  Pallas kernels  45.3 us (98%)
  between operations  0.64 us (1%)
    pallas_call x1, Pallas kernels, fused_body(): pl.pallas_call(functools.partial(kernel, shards, groups, grad_scale), nam...  44.2 us
    pallas_call x1, Pallas kernels, fused_body(): pl.pallas_call(place_outputs, name='place_outputs', out_shape=tuple((jax....  1.09 us

profile of v2, /device:TPU:0, one launch (start us, length us, event | category | flops | bytes accessed | tf_op | source)
XLA Modules:
  0.0 46.0 jit_solution(11254199352499621313)
XLA Ops:
  0.6 44.2 %projector_backward.1 = (bf16[96,4096]{1,0:T(8,128)(2,1)S(1)}, f32[1024,128]{1,0:T(8,128)S(1)}) custom-call(s32[4]{0:T(128)} %count_ref.1, bf16[1024,128]{1,0:T(8,128)(2,1)} %proj_hbm.1, bf16[128,1024]{1,0:T(8,128)(2,1)} %vision_hbm.1, f32[1,4096]{1,0:T(1,128)} %bitcast.3, bf16[512,1024]{1,0:T(8,128)(2,1)} %q_hbm.1, bf16[4,1024,1024]{2,1,0:T(8,128)(2,1)} %bitcast.2, ...), custom_call_target="tpu_custom_call" | custom-call | tf_op jit(solution)/shard_map/projector_backward/pallas_call | solution.py:581
  44.9 1.1 %place_outputs.1 = (bf16[96,4096]{1,0:T(8,128)(2,1)}, f32[1024,128]{1,0:T(8,128)}) custom-call(bf16[96,4096]{1,0:T(8,128)(2,1)S(1)} %get-tuple-element.4.text_in, f32[1024,128]{1,0:T(8,128)S(1)} %get-tuple-element.5.proj_in), custom_call_target="tpu_custom_call" | custom-call | tf_op jit(solution)/shard_map/place_outputs/pallas_call | solution.py:637

commit v3 on v2

--- a/solution.py
+++ b/solution.py
@@ -15,6 +15,7 @@
 CHUNKS = 4
 PIECES = 2
 LANES = 128
+TILE = 512
 ROW_STEP = 16
 
 MESH = pl.DeviceIdType.MESH
@@ -178,7 +179,7 @@
     far = [lax.rem(y + step, chips) for step in range(1, chips)]
     order = [yy * CORES + lax.rem(core + flip, CORES) for yy in far + [y] for flip in (1, 0)]
     early = len(order) - CORES
-    offsets = sorted(range(1, depth), key=lambda o: -min(o, depth - o)) + [0]
+    offsets = list(range(1, depth)) + [0]
     targets = [
         lax.rem(z + o, depth) * SIDE + (x if flip else 1 - x) for o in offsets for flip in (0, 1)
     ]
@@ -300,20 +301,22 @@
         j = order[k]
         w_copies[k].wait()
 
-        @pl.loop(0, 1)
+        @pl.loop(0, bc // TILE)
         def _(n):
-            rows = pl.ds(pl.multiple_of(n * bc, bc), bc)
+            rows = pl.ds(pl.multiple_of(n * TILE, TILE), TILE)
             own_image[j, rows] = row_term(wv[j, rows], q_image[...]).astype(bf16)
 
         if k % CORES == 0:
             image_to_mate((far + [y])[k // CORES]).start()
 
-    def text_multiply(k):
+    def text_multiply(k, part, parts):
         j = order[k]
-        term = row_term(q_text[...], wv[j]).astype(bf16)
+        cols = slice(part * bc // parts, (part + 1) * bc // parts)
+        term = row_term(q_text[...], wv[j, cols]).astype(bf16)
         for g in range(groups):
-            own_text[j, g % CORES, g // CORES] = term[g * text_rows : (g + 1) * text_rows]
-        text_to_mate(k).start()
+            own_text[j, g % CORES, g // CORES, :, cols] = term[g * text_rows : (g + 1) * text_rows]
+        if part == parts - 1:
+            text_to_mate(k).start()
 
     def add_image(yy):
         image_to_mate(yy).wait_recv()
@@ -372,7 +375,21 @@
 
     images = [functools.partial(spread_image, t) for t in range(shards)]
 
-    first, rest = each(vision.relay, 1)[:2], each(vision.relay, 1)[2:]
+    def part(k, h):
+        return functools.partial(text_multiply, k, h, 2)
+
+    def send_w(early):
+        for t in range(last):
+            level = targets[t] // SIDE
+            near = jnp.where(z < depth // 2, level == z + 1, level == z - 1)
+
+            @pl.when(near if early else jnp.logical_not(near))
+            def _():
+                w_to(t).start()
+
+    hops = [None] + [each(vision.relay, hop) for hop in range(1, depth)]
+    sides = [each(vision.side, hop) for hop in range(depth)]
+
     q_image_done.wait()
     for k in range(len(order)):
         image_multiply(k)
@@ -381,33 +398,28 @@
         if k % CORES == 0 and k >= CORES:
             add_image(far[k // CORES - 1])
             if k == CORES:
-                play(*first)
+                play(*hops[1][:1])
     for hop in range(min(len(order) + 1, depth - 1), depth):
         pass_on(hop)
-    play(*rest)
-    for t in range(last):
-        w_to(t).start()
     q_text_done.wait()
-    text_multiply(0)
-    play(*each(vision.side, 0))
-    play(*images[:1])
-    text_multiply(1)
-    play(*images[1:2])
+    play(hops[1][1], part(0, 0), hops[1][2], part(0, 1), *hops[1][3:])
+    send_w(True)
+    play(*sides[0])
+    play(hops[2][0], part(1, 0), *hops[2][1:3], part(1, 1), *hops[2][3:])
+    send_w(False)
+    play(*images[:4])
     add_text(0)
-    waves = [each(vision.relay, hop) for hop in range(2, depth)]
-    flow = [action for wave in waves for action in wave]
-    for k in range(2, len(order)):
-        text_multiply(k)
-        play(*images[2 * k - 2 : 2 * k])
-        play(*flow[2 * k - 4 : 2 * k - 2])
-        if k == 2:
-            add_text(1)
-    play(*images[2 * len(order) - 2 :])
+    add_text(1)
+    play(part(2, 0), *images[4:6], part(2, 1), *images[6:], part(3, 0), part(3, 1))
+    for k in range(4, len(order)):
+        play(part(k, 0), part(k, 1))
     gain_copy.wait()
     own_gain = gain_ref[:, pl.ds(pl.multiple_of(member * bc + me * span, span), span)]
     gain_t[...] = jnp.broadcast_to(own_gain, (image_rows, span)).T
-    play(*each(vision.side, 1))
-    play(*flow[2 * len(order) - 4 :])
+    play(*sides[1])
+    for hop in range(3, depth):
+        for chunk in range(CHUNKS):
+            play(hops[hop][chunk], sides[hop - 1][chunk])
     all_to(w_out, wt_send, wt_recv).wait_recv()
 
     def embed(zz):
@@ -420,12 +432,11 @@
         for s in range(SIDE):
             stat_f32[pl.ds(zz * SIDE + s, 1)] = squares[:, s * image_rows : (s + 1) * image_rows]
 
-    for hop in range(depth):
-        if hop >= 2:
-            play(*each(vision.side, hop))
-        if hop < depth - 1:
-            vision.levels(hop, embed)
-    vision.levels(depth - 1, embed)
+    for hop in range(depth - 2):
+        vision.levels(hop, embed)
+    play(*sides[depth - 1])
+    for hop in range(depth - 2, depth):
+        vision.levels(hop, embed)
 
     all_to(n_out, n_send, n_recv).wait_recv()
     for j in range(shards):
@@ -711,13 +722,14 @@
         count % bc == 0
         and shard_k == LANES
         and bc == shards * LANES
+        and bc % TILE == 0
         and shard_k * shards == vision_rows.shape[1]
         and shard_k == vision_rows.shape[0]
-        and groups > CORES
+        and groups == 2 * CORES
         and groups % CORES == 0
         and vision_rows.shape[0] // groups % ROW_STEP == 0
         and text_embeds.shape[0] % (PIECES * ROW_STEP) == 0
-        and shards > SIDE
+        and shards > 2 * SIDE
         and shards % SIDE == 0
     )
     run = fused_body if fits else general_body

time: 46.1 us -> 43.1 us (0.935)
  Pallas kernels: 45.3 us -> 42.2 us
    pallas_call x1, Pallas kernels: 44.2 us -> 41.2 us  [fused_body(): pl.pallas_call(functools.partial(kernel, shards, groups, grad_scale), nam...]
where the time goes in v3:
time: 43.1 us; the launch traced here: 42.9 us
  Pallas kernels  42.2 us (98%)
  between operations  0.64 us (1%)
    pallas_call x1, Pallas kernels, fused_body(): pl.pallas_call(functools.partial(kernel, shards, groups, grad_scale), nam...  41.2 us
    pallas_call x1, Pallas kernels, fused_body(): pl.pallas_call(place_outputs, name='place_outputs', out_shape=tuple((jax....  1.09 us

profile of v3, /device:TPU:0, one launch (start us, length us, event | category | flops | bytes accessed | tf_op | source)
XLA Modules:
  0.0 42.9 jit_solution(639282039586149291)
XLA Ops:
  0.6 41.2 %projector_backward.1 = (bf16[96,4096]{1,0:T(8,128)(2,1)S(1)}, f32[1024,128]{1,0:T(8,128)S(1)}) custom-call(s32[4]{0:T(128)} %count_ref.1, bf16[1024,128]{1,0:T(8,128)(2,1)} %proj_hbm.1, bf16[128,1024]{1,0:T(8,128)(2,1)} %vision_hbm.1, f32[1,4096]{1,0:T(1,128)} %bitcast.3, bf16[512,1024]{1,0:T(8,128)(2,1)} %q_hbm.1, bf16[4,1024,1024]{2,1,0:T(8,128)(2,1)} %bitcast.2, ...), custom_call_target="tpu_custom_call" | custom-call | tf_op jit(solution)/shard_map/projector_backward/pallas_call | solution.py:592
  41.8 1.1 %place_outputs.1 = (bf16[96,4096]{1,0:T(8,128)(2,1)}, f32[1024,128]{1,0:T(8,128)}) custom-call(bf16[96,4096]{1,0:T(8,128)(2,1)S(1)} %get-tuple-element.4.text_in, f32[1024,128]{1,0:T(8,128)S(1)} %get-tuple-element.5.proj_in), custom_call_target="tpu_custom_call" | custom-call | tf_op jit(solution)/shard_map/place_outputs/pallas_call | solution.py:648

commit v4 on v3

--- a/solution.py
+++ b/solution.py
@@ -185,11 +185,27 @@
     ]
     last = shards - 1
 
-    p_copy = pltpu.make_async_copy(proj_hbm, pv, p_sem)
-    p_copy.start()
+    barrier = pltpu.get_barrier_semaphore()
+    across = z * SIDE + 1 - x
+    beside = [(me, lax.rem(member + step, groups)) for step in range(1, groups)]
+    beside += [(across, lax.rem(member + step, groups)) for step in range(groups)]
+    greeted = beside[: groups - 1] + [(across, member)]
+    for device in greeted:
+        pl.semaphore_signal(barrier, inc=1, device_id=device, device_id_type=MESH)
+
+    @pl.when(z > 0)
+    def _():
+        pl.semaphore_signal(barrier, inc=1, device_id=(me - SIDE, member), device_id_type=MESH)
+
+    @pl.when(z < depth - 1)
+    def _():
+        pl.semaphore_signal(barrier, inc=1, device_id=(me + SIDE, member), device_id_type=MESH)
+
     own_rows = pl.ds(pl.multiple_of(me * image_rows, image_rows), image_rows)
     vis_copy = pltpu.make_async_copy(vision_hbm, vv.at[own_rows], vis_sem)
     vis_copy.start()
+    p_copy = pltpu.make_async_copy(proj_hbm, pv, p_sem)
+    p_copy.start()
     q_copies = [
         pltpu.make_async_copy(
             q_hbm.at[pl.ds(g * rows_dev + first, count)], dst.at[pl.ds(g * count, count)], q_sem.at[k]
@@ -205,21 +221,6 @@
     for copy in q_copies[:groups] + w_copies[:1]:
         copy.start()
 
-    barrier = pltpu.get_barrier_semaphore()
-    across = z * SIDE + 1 - x
-    beside = [(me, lax.rem(member + step, groups)) for step in range(1, groups)]
-    beside += [(across, lax.rem(member + step, groups)) for step in range(groups)]
-    for device in beside:
-        pl.semaphore_signal(barrier, inc=1, device_id=device, device_id_type=MESH)
-
-    @pl.when(z > 0)
-    def _():
-        pl.semaphore_signal(barrier, inc=1, device_id=(me - SIDE, member), device_id_type=MESH)
-
-    @pl.when(z < depth - 1)
-    def _():
-        pl.semaphore_signal(barrier, inc=1, device_id=(me + SIDE, member), device_id_type=MESH)
-
     def pass_on(hop):
         @pl.when(z == hop)
         def _():
@@ -241,11 +242,11 @@
 
     @pl.when((z == 0) | (z == depth - 1))
     def _():
-        pl.semaphore_wait(barrier, len(beside) + 1)
+        pl.semaphore_wait(barrier, len(greeted) + 1)
 
     @pl.when((z > 0) & (z < depth - 1))
     def _():
-        pl.semaphore_wait(barrier, len(beside) + 2)
+        pl.semaphore_wait(barrier, len(greeted) + 2)
 
     vision = VisionGather(depth, me, member, vv, image_rows, v_send, v_recv, vm_send, vm_recv)
     vision.start()
@@ -266,6 +267,20 @@
         place = buf.at[pl.ds(0, last)]
         return remote(place, place, send, recv, (me, mate))
 
+    def send_w(stage):
+        for t in range(last):
+            level = targets[t] // SIDE
+            outward = jnp.where(z < depth // 2, z + 1, z - 1)
+            straight = (level == z) | ((level - z) * (level - z) == 1) & (targets[t] % SIDE == x)
+            aside = jnp.logical_not(straight) & (level == outward)
+            due = (straight, aside, jnp.logical_not(straight | aside))[stage]
+
+            @pl.when(due)
+            def _():
+                w_to(t).start()
+
+    send_w(0)
+
     def text_to_mate(k):
         j = order[k]
         return remote(own_text.at[j, 1 - core], mate_text.at[j], mt_send, mt_recv.at[j], (me, mate))
@@ -288,13 +303,13 @@
     def image_to_far(yy, t):
         return remote(
             sum_image.at[yy, piece(t)], far_image.at[y, piece(t)],
-            fi_send, fi_recv.at[y, t], (me, yy * CORES + core),
+            fi_send, fi_recv.at[t], (me, yy * CORES + core),
         )
 
     def image_from_far(yy, t):
         return remote(
             sum_image.at[yy, piece(t)], far_image.at[yy, piece(t)],
-            fi_send, fi_recv.at[yy, t], (me, yy * CORES + core),
+            fi_send, fi_recv.at[t], (me, yy * CORES + core),
         )
 
     def image_multiply(k):
@@ -378,15 +393,6 @@
     def part(k, h):
         return functools.partial(text_multiply, k, h, 2)
 
-    def send_w(early):
-        for t in range(last):
-            level = targets[t] // SIDE
-            near = jnp.where(z < depth // 2, level == z + 1, level == z - 1)
-
-            @pl.when(near if early else jnp.logical_not(near))
-            def _():
-                w_to(t).start()
-
     hops = [None] + [each(vision.relay, hop) for hop in range(1, depth)]
     sides = [each(vision.side, hop) for hop in range(depth)]
 
@@ -403,10 +409,10 @@
         pass_on(hop)
     q_text_done.wait()
     play(hops[1][1], part(0, 0), hops[1][2], part(0, 1), *hops[1][3:])
-    send_w(True)
+    send_w(1)
     play(*sides[0])
     play(hops[2][0], part(1, 0), *hops[2][1:3], part(1, 1), *hops[2][3:])
-    send_w(False)
+    send_w(2)
     play(*images[:4])
     add_text(0)
     add_text(1)
@@ -548,7 +554,7 @@
     remote(mate_text, mate_text, mt_send, mt_recv.at[0], (me, mate)).wait_send()
     remote(mate_image, mate_image, mi_send, mi_recv.at[0], (me, mate)).wait_send()
     image_far = sum_image.at[pl.ds(0, len(far))]
-    remote(image_far, image_far, fi_send, fi_recv.at[0, 0], (me, mate)).wait_send()
+    remote(image_far, image_far, fi_send, fi_recv.at[0], (me, mate)).wait_send()
 
 
 def place_outputs(text_in, proj_in, text_out, proj_out, sem):
@@ -629,7 +635,7 @@
             dma, dma, dma, dma((2,)), dma((groups,)), dma,
             dma((3,)), dma((shards, CHUNKS)), dma, dma((shards,)),
             dma, dma, dma, dma, dma, dma((shards,)),
-            dma, dma((groups,)), dma, dma((chips,)), dma, dma, dma, dma((chips, shards)),
+            dma, dma((groups,)), dma, dma((chips,)), dma, dma, dma, dma((shards,)),
             dma, dma, dma, dma, pltpu.SemaphoreType.REGULAR, pltpu.SemaphoreType.REGULAR,
         ],
         compiler_params=pltpu.CompilerParams(

time: 43.1 us -> 42.7 us (level)
  no operation moved by 1% of the time
where the time goes in v4:
time: 42.7 us; the launch traced here: 42.5 us
  Pallas kernels  41.9 us (98%)
  between operations  0.64 us (1%)
    pallas_call x1, Pallas kernels, fused_body(): pl.pallas_call(functools.partial(kernel, shards, groups, grad_scale), nam...  40.8 us
    pallas_call x1, Pallas kernels, fused_body(): pl.pallas_call(place_outputs, name='place_outputs', out_shape=tuple((jax....  1.09 us

profile of v4, /device:TPU:0, one launch (start us, length us, event | category | flops | bytes accessed | tf_op | source)
XLA Modules:
  0.0 42.5 jit_solution(10212022507803523577)
XLA Ops:
  0.6 40.8 %projector_backward.1 = (bf16[96,4096]{1,0:T(8,128)(2,1)S(1)}, f32[1024,128]{1,0:T(8,128)S(1)}) custom-call(s32[4]{0:T(128)} %count_ref.1, bf16[1024,128]{1,0:T(8,128)(2,1)} %proj_hbm.1, bf16[128,1024]{1,0:T(8,128)(2,1)} %vision_hbm.1, f32[1,4096]{1,0:T(1,128)} %bitcast.3, bf16[512,1024]{1,0:T(8,128)(2,1)} %q_hbm.1, bf16[4,1024,1024]{2,1,0:T(8,128)(2,1)} %bitcast.2, ...), custom_call_target="tpu_custom_call" | custom-call | tf_op jit(solution)/shard_map/projector_backward/pallas_call | solution.py:598
  41.4 1.1 %place_outputs.1 = (bf16[96,4096]{1,0:T(8,128)(2,1)}, f32[1024,128]{1,0:T(8,128)}) custom-call(bf16[96,4096]{1,0:T(8,128)(2,1)S(1)} %get-tuple-element.4.text_in, f32[1024,128]{1,0:T(8,128)S(1)} %get-tuple-element.5.proj_in), custom_call_target="tpu_custom_call" | custom-call | tf_op jit(solution)/shard_map/place_outputs/pallas_call | solution.py:654

commit v5 on v4

--- a/solution.py
+++ b/solution.py
@@ -416,13 +416,12 @@
     play(*images[:4])
     add_text(0)
     add_text(1)
-    play(part(2, 0), *images[4:6], part(2, 1), *images[6:], part(3, 0), part(3, 1))
+    play(part(2, 0), *images[4:6], part(2, 1), *images[6:], *sides[1], part(3, 0), part(3, 1))
     for k in range(4, len(order)):
         play(part(k, 0), part(k, 1))
     gain_copy.wait()
     own_gain = gain_ref[:, pl.ds(pl.multiple_of(member * bc + me * span, span), span)]
     gain_t[...] = jnp.broadcast_to(own_gain, (image_rows, span)).T
-    play(*sides[1])
     for hop in range(3, depth):
         for chunk in range(CHUNKS):
             play(hops[hop][chunk], sides[hop - 1][chunk])

time: 42.7 us -> 42.7 us (level)
  no operation moved by 1% of the time
where the time goes in v5:
time: 42.7 us; the launch traced here: 42.5 us
  Pallas kernels  41.9 us (98%)
  between operations  0.64 us (1%)
    pallas_call x1, Pallas kernels, fused_body(): pl.pallas_call(functools.partial(kernel, shards, groups, grad_scale), nam...  40.8 us
    pallas_call x1, Pallas kernels, fused_body(): pl.pallas_call(place_outputs, name='place_outputs', out_shape=tuple((jax....  1.09 us

profile of v5, /device:TPU:0, one launch (start us, length us, event | category | flops | bytes accessed | tf_op | source)
XLA Modules:
  0.0 42.5 jit_solution(7950533859093782022)
XLA Ops:
  0.6 40.8 %projector_backward.1 = (bf16[96,4096]{1,0:T(8,128)(2,1)S(1)}, f32[1024,128]{1,0:T(8,128)S(1)}) custom-call(s32[4]{0:T(128)} %count_ref.1, bf16[1024,128]{1,0:T(8,128)(2,1)} %proj_hbm.1, bf16[128,1024]{1,0:T(8,128)(2,1)} %vision_hbm.1, f32[1,4096]{1,0:T(1,128)} %bitcast.3, bf16[512,1024]{1,0:T(8,128)(2,1)} %q_hbm.1, bf16[4,1024,1024]{2,1,0:T(8,128)(2,1)} %bitcast.2, ...), custom_call_target="tpu_custom_call" | custom-call | tf_op jit(solution)/shard_map/projector_backward/pallas_call | solution.py:597
  41.4 1.1 %place_outputs.1 = (bf16[96,4096]{1,0:T(8,128)(2,1)}, f32[1024,128]{1,0:T(8,128)}) custom-call(bf16[96,4096]{1,0:T(8,128)(2,1)S(1)} %get-tuple-element.4.text_in, f32[1024,128]{1,0:T(8,128)S(1)} %get-tuple-element.5.proj_in), custom_call_target="tpu_custom_call" | custom-call | tf_op jit(solution)/shard_map/place_outputs/pallas_call | solution.py:653
